TPU v7x, 8 devices: a whole 2x2x1 slice. The times are simulated.
8 devices in a mesh: fsdp: 2 (over z, y), ep: 4 (over x, core).
Axes of the slice: x: 2, y: 2, z: 1, core: 2. Of those that a mesh axis runs over, the one named last changes fastest.
Arguments:
- grad_out: bfloat16 [16384, 768], P(('fsdp', 'ep'))
- expert_idx: int32 [16384, 1], P(('fsdp', 'ep'))
- slot_pos: int32 [16384, 1], P(('fsdp', 'ep'))
- gates: float32 [16384, 1], P(('fsdp', 'ep'))
- x_disp: bfloat16 [8, 2560, 768], P('ep', 'fsdp')
- h_gate: bfloat16 [8, 2560, 3072], P('ep', 'fsdp')
- h_up: bfloat16 [8, 2560, 3072], P('ep', 'fsdp')
- y_disp: bfloat16 [8, 2560, 768], P('ep', 'fsdp')
- w_gate: bfloat16 [8, 768, 3072], P('ep', 'fsdp')
- w_down: bfloat16 [8, 3072, 768], P('ep', 'fsdp')
- w_up: bfloat16 [8, 768, 3072], P('ep', 'fsdp')
Outputs:
- output 1: bfloat16 [16384, 768], P(('fsdp', 'ep'))
- output 2: float32 [16384, 1], P(('fsdp', 'ep'))
- output 3: float32 [8, 768, 3072], P('ep', 'fsdp')
- output 4: float32 [8, 3072, 768], P('ep', 'fsdp')
- output 5: float32 [8, 768, 3072], P('ep', 'fsdp')
All inputs are finite; a program needn't handle non-finite values.
Results may differ from a plain program's by a relative error of at most 0.001.
Values are sent between devices in bfloat16 or wider.
A program may use at most 1 GiB of HBM per device.

v0:
```python
import jax
import jax.numpy as jnp
from jax import lax
from jax.sharding import PartitionSpec as P


def expert_grads(dy_rows, gate_rows, x_rows, h_gate, h_up, y_rows, w_gate, w_down, w_up):
    g_rows = (dy_rows.astype(jnp.float32) * gate_rows[..., None]).astype(jnp.bfloat16)
    gate_pre = h_gate.astype(jnp.float32)
    up_pre = h_up.astype(jnp.float32)
    sigmoid_gate = jax.nn.sigmoid(gate_pre)
    silu_gate = gate_pre * sigmoid_gate
    act_rows = (silu_gate * up_pre).astype(jnp.bfloat16)
    d_act = jnp.einsum('erd,efd->erf', g_rows, w_down, preferred_element_type=jnp.float32)
    dh_gate = (d_act * up_pre * sigmoid_gate * (1.0 + gate_pre * (1.0 - sigmoid_gate))).astype(jnp.bfloat16)
    dh_up = (d_act * silu_gate).astype(jnp.bfloat16)
    dx_rows = (jnp.einsum('erf,edf->erd', dh_gate, w_gate, preferred_element_type=jnp.float32) + jnp.einsum('erf,edf->erd', dh_up, w_up, preferred_element_type=jnp.float32)).astype(jnp.bfloat16)
    dgate_rows = jnp.einsum('erd,erd->er', dy_rows, y_rows, preferred_element_type=jnp.float32)
    dw_gate = jnp.einsum('erd,erf->edf', x_rows, dh_gate, preferred_element_type=jnp.float32)
    dw_down = jnp.einsum('erf,erd->efd', act_rows, g_rows, preferred_element_type=jnp.float32)
    dw_up = jnp.einsum('erd,erf->edf', x_rows, dh_up, preferred_element_type=jnp.float32)
    return dx_rows, dgate_rows, dw_gate, dw_down, dw_up


def solution(mesh):
    ep_n = mesh.shape['ep']
    tok_spec = P(('fsdp', 'ep'), None)
    row_spec = P('ep', 'fsdp', None)

    def local_backward(grad_out, expert_idx, slot_pos, gates, x_disp, h_gate, h_up, y_disp, w_gate, w_down, w_up):
        tok_n, top_n = expert_idx.shape
        e_loc, rows_loc, width = x_disp.shape
        slot_cap = rows_loc // ep_n
        slots_n = e_loc * ep_n * slot_cap
        choices = tok_n * top_n
        send_row = jnp.where(slot_pos >= 0, ((expert_idx % e_loc) * ep_n + expert_idx // e_loc) * slot_cap + slot_pos, slots_n).reshape(-1)
        src_choice = jnp.full((slots_n,), choices, jnp.int32).at[send_row].set(jnp.arange(choices, dtype=jnp.int32), mode='drop')
        send_dy = jnp.take(grad_out, src_choice // top_n, axis=0, mode='fill', fill_value=0).reshape(e_loc, ep_n, slot_cap, width)
        send_gate = jnp.take(gates.reshape(-1), src_choice, mode='fill', fill_value=0).reshape(e_loc, ep_n, slot_cap)
        recv_dy = lax.all_to_all(send_dy, 'ep', 1, 1, tiled=True).reshape(e_loc, rows_loc, width)
        recv_gate = lax.all_to_all(send_gate, 'ep', 1, 1, tiled=True).reshape(e_loc, rows_loc)
        full_w_gate = lax.all_gather(w_gate, 'fsdp', axis=1, tiled=True)
        full_w_down = lax.all_gather(w_down, 'fsdp', axis=1, tiled=True)
        full_w_up = lax.all_gather(w_up, 'fsdp', axis=1, tiled=True)
        dx_rows, dgate_rows, dw_gate, dw_down, dw_up = expert_grads(recv_dy, recv_gate, x_disp, h_gate, h_up, y_disp, full_w_gate, full_w_down, full_w_up)
        back_dx = lax.all_to_all(dx_rows.reshape(e_loc, ep_n, slot_cap, width), 'ep', 1, 1, tiled=True).reshape(slots_n, width)
        back_gate = lax.all_to_all(dgate_rows.reshape(e_loc, ep_n, slot_cap), 'ep', 1, 1, tiled=True).reshape(slots_n)
        picked = jnp.take(back_dx, send_row, axis=0, mode='fill', fill_value=0).reshape(tok_n, top_n, width)
        grad_x = jnp.sum(picked.astype(jnp.float32), axis=1).astype(jnp.bfloat16)
        grad_gates = jnp.take(back_gate, send_row, mode='fill', fill_value=0).reshape(tok_n, top_n)
        grad_w_gate = lax.psum_scatter(dw_gate, 'fsdp', scatter_dimension=1, tiled=True)
        grad_w_down = lax.psum_scatter(dw_down, 'fsdp', scatter_dimension=1, tiled=True)
        grad_w_up = lax.psum_scatter(dw_up, 'fsdp', scatter_dimension=1, tiled=True)
        return grad_x, grad_gates, grad_w_gate, grad_w_down, grad_w_up

    return jax.shard_map(local_backward, mesh=mesh, in_specs=(tok_spec, tok_spec, tok_spec, tok_spec, row_spec, row_spec, row_spec, row_spec, row_spec, row_spec, row_spec), out_specs=(tok_spec, tok_spec, row_spec, row_spec, row_spec), check_vma=False)
```

profile of v0, /device:TPU:0, one launch (start us, length us, event | category | flops | bytes accessed | tf_op | source)
XLA Modules:
  0.0 996.9 jit_solution(11296085855768351572)
XLA Ops:
  9.4 8.1 scatter_custom_fusion
  17.6 13.6 %gather_fusion.1 = f32[2560]{0:T(1024)S(1)} fusion(f32[2048]{0:T(1024)S(1)} %bitcast.24, s32[3072]{0:T(1024)S(1)} %pad_clamp_fusion), kind=kCustom, calls=%fused_computation.1 | custom fusion | bytes 30720 | tf_op jit(solution)/shard_map/jit(_take)/gather | solution.py:39
  31.9 4.6 all-to-all-start.1
  36.6 8.5 gather_fusion
  45.1 3.7 copy_select_fusion
  48.8 4.8 all-to-all-start
  54.5 44.2 %all-to-all-done = bf16[2,4,320,768]{3,2,0,1:T(8,128)(2,1)} async-done(((bf16[2,4,320,768]{3,2,0,1:T(8,128)(2,1)}), bf16[2,4,320,768]{3,2,0,1:T(8,128)(2,1)}, u32[]{:S(2)}, u32[]{:S(2)}) %all-to-all-start) | async-done | bytes 3932192 | tf_op jit(solution)/shard_map/all_to_all | solution.py:40
  98.7 2.5 copy.36
  101.3 0.8 copy-done.3
  102.0 4.2 fusion.11
  106.3 19.6 %all-gather.4.cloned.1.call-done = bf16[2,3072,768]{2,1,0:T(8,128)(2,1)} async-done(((bf16[2,1536,768]{2,1,0:T(8,128)(2,1)}), bf16[2,3072,768]{2,1,0:T(8,128)(2,1)}) %all-gather.4.cloned.1.call-update) | async-done | bytes 9437200 | tf_op jit(solution)/shard_map/all_gather | solution.py:43
  125.9 33.1 %multiply_convert_fusion = (bf16[2,1280,3072]{2,1,0:T(8,128)(2,1)}, bf16[2,1280,3072]{2,1,0:T(8,128)(2,1)}) fusion(bf16[2,1280,3072]{2,1,0:T(8,128)(2,1)} %param.16, bf16[2,1280,3072]{2,1,0:T(8,128)(2,1)} %param.17, bf16[2,1280,768]{2,1,0:T(8,128)(2,1)} %get-tuple-element.30, bf16[2,3072,768]{2,1,0:T(8,128)(2,1)} %all-gather.4.cloned.1.call-done), kind=kOutput, calls=%fused_computation.18 | convolution fusion | flops 12197560320 | bytes 76283904 | tf_op jit(solution)/shard_map/erd,efd->erf/dot_general | solution.py:14
  159.0 21.3 %convolution_bitcast_fusion.1 = f32[2,768,3072]{1,2,0:T(8,128)} fusion(bf16[2,1280,3072]{2,1,0:T(8,128)(2,1)} %get-tuple-element.28, bf16[2,1280,768]{2,1,0:T(8,128)(2,1)} %param.15), kind=kOutput, calls=%fused_computation.23 | convolution fusion | flops 12079595520 | bytes 38535168 | tf_op jit(solution)/shard_map/erd,erf->edf/dot_general | solution.py:19
  180.4 21.1 %convolution_bitcast_fusion = f32[2,768,3072]{1,2,0:T(8,128)} fusion(bf16[2,1280,3072]{2,1,0:T(8,128)(2,1)} %get-tuple-element.27, bf16[2,1280,768]{2,1,0:T(8,128)(2,1)} %param.15), kind=kOutput, calls=%fused_computation.22 | convolution fusion | flops 12079595520 | bytes 38535168 | tf_op jit(solution)/shard_map/erd,erf->edf/dot_general | solution.py:21
  201.6 28.2 %fusion.8 = f32[2,3072,768]{2,1,0:T(8,128)} fusion(bf16[2,1280,768]{2,1,0:T(8,128)(2,1)} %get-tuple-element.30, bf16[2,1280,3072]{2,1,0:T(8,128)(2,1)} %param.17, bf16[2,1280,3072]{2,1,0:T(8,128)(2,1)} %param.16), kind=kOutput, calls=%fused_computation.19 | convolution fusion | flops 12142510080 | bytes 54263808 | tf_op jit(solution)/shard_map/erf,erd->efd/dot_general | solution.py:20
  231.2 3.5 all-to-all-start.3
  234.7 6.2 all-gather.6.cloned.1.call-done
  240.9 19.7 %fusion.18 = f32[2,1280,768]{2,1,0:T(8,128)} fusion(bf16[2,1280,3072]{2,1,0:T(8,128)(2,1)} %get-tuple-element.28, bf16[2,768,3072]{2,1,0:T(8,128)(2,1)} %all-gather.6.cloned.1.call-done), kind=kOutput, calls=%fused_computation.49 | convolution fusion | flops 12079595520 | bytes 33030144 | tf_op jit(solution)/shard_map/erf,edf->erd/dot_general | solution.py:17
  260.6 95.3 %all-gather.8.cloned.1.call-done = bf16[2,768,3072]{2,1,0:T(8,128)(2,1)} async-done(((bf16[2,384,3072]{2,1,0:T(8,128)(2,1)}), bf16[2,768,3072]{2,1,0:T(8,128)(2,1)}) %all-gather.8.cloned.1.call-update) | async-done | bytes 9437200 | tf_op jit(solution)/shard_map/all_gather | solution.py:44
  355.9 20.9 %add_convert_fusion = bf16[2,1280,768]{2,1,0:T(8,128)(2,1)} fusion(f32[2,1280,768]{2,1,0:T(8,128)} %fusion.18, bf16[2,1280,3072]{2,1,0:T(8,128)(2,1)} %get-tuple-element.27, bf16[2,768,3072]{2,1,0:T(8,128)(2,1)} %all-gather.8.cloned.1.call-done), kind=kOutput, calls=%fused_computation.26 | convolution fusion | flops 12083527680 | bytes 36962304 | tf_op jit(solution)/shard_map/erf,edf->erd/dot_general | solution.py:17
  376.8 4.3 copy.39
  381.1 5.1 all-to-all-start.2
  386.3 11.8 %gather_fusion.3 = f32[2048]{0:T(1024)S(1)} fusion(f32[2560]{0:T(1024)S(1)} %reshape.71, s32[2048]{0:T(1024)S(1)} %broadcast_clamp_fusion), kind=kCustom, calls=%fused_computation.3 | custom fusion | bytes 24576 | tf_op jit(solution)/shard_map/jit(_take)/gather | solution.py:50
  398.7 32.5 %all-to-all-done.2 = bf16[2,4,320,768]{3,2,0,1:T(8,128)(2,1)} async-done(((bf16[2,4,320,768]{3,2,0,1:T(8,128)(2,1)}), bf16[2,4,320,768]{3,2,0,1:T(8,128)(2,1)}, u32[]{:S(2)}, u32[]{:S(2)}) %all-to-all-start.2) | async-done | bytes 3932192 | tf_op jit(solution)/shard_map/all_to_all | solution.py:46
  431.3 4.3 copy.40
  435.6 11.1 %gather_fusion.2 = bf16[2048,768]{1,0:T(8,128)(2,1)S(1)} fusion(bf16[2560,768]{1,0:T(8,128)(2,1)} %bitcast.25, s32[2048]{0:T(1024)S(1)} %broadcast_clamp_fusion), kind=kCustom, calls=%fused_computation.2 | custom fusion | bytes 6299648 | tf_op jit(solution)/shard_map/jit(_take)/gather | solution.py:48
  446.7 1.9 broadcast_select_fusion
  448.6 118.4 %reduce-scatter.4.cloned.1.call-done = f32[2,384,3072]{1,2,0:T(8,128)} async-done(((f32[2,768,3072]{1,2,0:T(8,128)}), f32[2,384,3072]{1,2,0:T(8,128)}) %reduce-scatter.4.cloned.1.call-update) | async-done | bytes 9437200 | tf_op jit(solution)/shard_map/reduce_scatter | solution.py:51
  567.0 9.7 copy.46
  576.7 201.3 %reduce-scatter.8.cloned.1.call-done = f32[2,384,3072]{1,2,0:T(8,128)} async-done(((f32[2,768,3072]{1,2,0:T(8,128)}), f32[2,384,3072]{1,2,0:T(8,128)}) %reduce-scatter.8.cloned.1.call-update) | async-done | bytes 9437200 | tf_op jit(solution)/shard_map/reduce_scatter | solution.py:53
  778.0 9.6 copy.47
  787.6 202.0 %reduce-scatter.6.cloned.1.call-done = f32[2,1536,768]{2,1,0:T(8,128)} async-done(((f32[2,3072,768]{2,1,0:T(8,128)}), f32[2,1536,768]{2,1,0:T(8,128)}) %reduce-scatter.6.cloned.1.call-update) | async-done | bytes 9437200 | tf_op jit(solution)/shard_map/reduce_scatter | solution.py:52
  (51 shorter events, 6.1 us)
Async XLA Ops:
  7.2 29.4 %copy-start = (bf16[2048,768]{1,0:T(8,128)(2,1)S(1)}, bf16[2048,768]{1,0:T(8,128)(2,1)}, u32[]{:S(2)}) copy-start(bf16[2048,768]{1,0:T(8,128)(2,1)} %param.11) | copy-start | bytes 9437188
  7.2 1.5 copy-start.9
  7.2 1.5 copy-start.8
  7.2 10.4 %copy-start.2 = (f32[2048,1]{0,1:T(1,128)S(1)}, f32[2048,1]{0,1:T(1,128)}, u32[]{:S(2)}) copy-start(f32[2048,1]{0,1:T(1,128)} %param.14) | copy-start | bytes 24580
  7.2 118.7 %all-gather.4.cloned.1.call-start = ((), (), s32[]{:S(2)}) async-start(), calls=%async_computation.7 | async-start | bytes 14155776 | tf_op jit(solution)/shard_map/all_gather | solution.py:43
  7.9 233.0 %all-gather.6.cloned.1.call-start = ((), (), s32[]{:S(2)}) async-start(), calls=%async_computation.8 | async-start | bytes 14155776 | tf_op jit(solution)/shard_map/all_gather | solution.py:42
  9.4 35.7 %copy-start.4 = (s32[2048,1]{0,1:T(1,128)}, s32[2048,1]{0,1:T(1,128)S(1)}, u32[]{:S(2)}) copy-start(s32[2048,1]{0,1:T(1,128)S(1)} %get-tuple-element.26) | copy-start | bytes 24580
  31.9 16.9 %all-to-all-start.1 = ((f32[2,4,320]{2,0,1:T(2,128)}), f32[2,4,320]{2,0,1:T(2,128)S(1)}, u32[]{:S(2)}, u32[]{:S(2)}) async-start(f32[2,4,320]{2,0,1:T(2,128)} %copy.37), calls=%async_computation.1 | async-start | bytes 24576 | tf_op jit(solution)/shard_map/all_to_all | solution.py:41
  48.8 49.9 %all-to-all-start = ((bf16[2,4,320,768]{3,2,0,1:T(8,128)(2,1)}), bf16[2,4,320,768]{3,2,0,1:T(8,128)(2,1)}, u32[]{:S(2)}, u32[]{:S(2)}) async-start(bf16[2,4,320,768]{3,2,0,1:T(8,128)(2,1)} %copy_select_fusion), calls=%async_computation | async-start | bytes 7864320 | tf_op jit(solution)/shard_map/all_to_all | solution.py:40
  53.6 302.3 %all-gather.8.cloned.1.call-start = ((), (), s32[]{:S(2)}) async-start(), calls=%async_computation.9 | async-start | bytes 14155776 | tf_op jit(solution)/shard_map/all_gather | solution.py:44
  54.4 512.6 %reduce-scatter.4.cloned.1.call-start = ((), (), s32[]{:S(2)}) async-start(), calls=%async_computation.10 | async-start | bytes 28311552 | tf_op jit(solution)/shard_map/reduce_scatter | solution.py:51
  98.7 3.3 copy-start.3
  180.3 597.7 %reduce-scatter.8.cloned.1.call-start = ((), (), s32[]{:S(2)}) async-start(), calls=%async_computation.12 | async-start | bytes 28311552 | tf_op jit(solution)/shard_map/reduce_scatter | solution.py:53
  201.5 788.1 %reduce-scatter.6.cloned.1.call-start = ((), (), s32[]{:S(2)}) async-start(), calls=%async_computation.11 | async-start | bytes 28311552 | tf_op jit(solution)/shard_map/reduce_scatter | solution.py:52
  229.8 0.7 copy-start.6
  231.2 150.0 %all-to-all-start.3 = ((f32[2,4,320]{2,0,1:T(2,128)}), f32[2,4,320]{2,0,1:T(2,128)S(1)}, u32[]{:S(2)}, u32[]{:S(2)}) async-start(f32[2,4,320]{2,0,1:T(2,128)} %copy.41), calls=%async_computation.3 | async-start | bytes 24576 | tf_op jit(solution)/shard_map/all_to_all | solution.py:47
  376.8 9.4 copy-start.5
  381.1 50.2 %all-to-all-start.2 = ((bf16[2,4,320,768]{3,2,0,1:T(8,128)(2,1)}), bf16[2,4,320,768]{3,2,0,1:T(8,128)(2,1)}, u32[]{:S(2)}, u32[]{:S(2)}) async-start(bf16[2,4,320,768]{3,2,0,1:T(8,128)(2,1)} %copy.39), calls=%async_computation.2 | async-start | bytes 7864320 | tf_op jit(solution)/shard_map/all_to_all | solution.py:46
  435.6 11.1 %copy-start.7 = (pred[2048]{0:T(1024)(128)(4,1)S(1)}, pred[2048]{0:T(1024)(128)(4,1)}, u32[]{:S(2)}) copy-start(pred[2048]{0:T(1024)(128)(4,1)} %get-tuple-element.25) | copy-start | bytes 6148
  567.0 422.6 %copy-start.1 = (bf16[2048,768]{1,0:T(8,128)(2,1)S(1)}, bf16[2048,768]{1,0:T(8,128)(2,1)}, u32[]{:S(2)}) copy-start(bf16[2048,768]{1,0:T(8,128)(2,1)} %param.11) | copy-start | bytes 9437188
Sparse Core Ops, SparseCore 0:
  9.5 116.2 all-gather.3
  127.4 113.4 all-gather.5
  242.4 113.4 all-gather.7
  358.1 208.8 reduce-scatter.3
  569.1 208.8 reduce-scatter.7
  780.7 208.8 reduce-scatter.5
where the time goes:
time: 1000 us; the launch traced here: 997 us
  waiting for transfers between devices  722 us (72%)
  matrix products  144 us (14%)
  local copies, waits for them, and re-layouts  86.6 us (9%)
  starting transfers between devices  18.3 us (2%)
  between operations  14.8 us (1%)
  other arithmetic  11.2 us (1%)
    reduce_scatter x1, waiting for transfers between devices, local_backward(): lax.psum_scatter(dw_down, 'fsdp', scatter_dimension=1, tiled=True)  202 us
    reduce_scatter x1, waiting for transfers between devices, local_backward(): grad_w_up = lax.psum_scatter(dw_up, 'fsdp', scatter_dimension=1, tiled=True)  201 us
    reduce_scatter x1, waiting for transfers between devices, local_backward(): lax.psum_scatter(dw_gate, 'fsdp', scatter_dimension=1, tiled=True)  118 us
    all_gather x1, waiting for transfers between devices, local_backward(): full_w_up = lax.all_gather(w_up, 'fsdp', axis=1, tiled=True)  95.3 us
    all_to_all x1, waiting for transfers between devices, local_backward(): lax.all_to_all(send_dy, 'ep', 1, 1, tiled=True)  44.2 us
    dot_general x1, matrix products, expert_grads(): jnp.einsum('erd,efd->erf', g_rows, w_down, preferred_element_type=jnp.flo...  33.1 us
    all_to_all x1, waiting for transfers between devices, local_backward(): lax.all_to_all(dx_rows.reshape(e_loc, ep_n, slot_cap, width), 'ep', 1, 1,...  32.5 us
    dot_general x1, matrix products, expert_grads(): jnp.einsum('erf,erd->efd', act_rows, g_rows, preferred_element_type=jnp.f...  28.2 us
  transfers between devices with their start and end apart: 10, of which 8 were waited for; matrix products, arithmetic and copies ran while one was open for 24% of the time, Pallas kernels for 0%

commit v1 on v0

v1 whole, which is shorter than its diff:
```python
import functools

import jax
import jax.numpy as jnp
from jax import lax
from jax.experimental import pallas as pl
from jax.experimental.pallas import tpu as pltpu
from jax.sharding import PartitionSpec as P

CHUNK = 128
UNIT = 8
TILE = 768
F32, BF16, I32 = jnp.float32, jnp.bfloat16, jnp.int32


def dot_nt(a, b):
    return lax.dot_general(a, b, (((1,), (1,)), ((), ())), preferred_element_type=F32)


def dot_tn(a, b):
    return lax.dot_general(a, b, (((0,), (0,)), ((), ())), preferred_element_type=F32)


def seg_tiles(tab, side, s):
    first = tab[side, s - 1] if s else 0
    return first, tab[side, s]


def touched(tab, i, e):
    segs = tab.shape[1] // 2
    lo, hi = i * (CHUNK // UNIT), (i + 1) * (CHUNK // UNIT)
    one = ((tab[0, segs // 2 - 1] < hi) & (tab[0, segs - 1] > lo)) | ((tab[1, segs // 2 - 1] < hi) & (tab[1, segs - 1] > lo))
    zero = (tab[0, segs // 2 - 1] > lo) | (tab[1, segs // 2 - 1] > lo) | jnp.logical_not(one)
    return jnp.where(e == 0, zero, one)


def expert_at(tab, i, turn):
    return jnp.where(touched(tab, i, 1), turn, 1 - turn)


def pack_kernel(tab, me, step, h1, h3, g, x, dx, out, keep, sems, dx_sem):
    segs = tab.shape[1] // 2
    all_units = h1.shape[0] // UNIT
    hid, width, w_half = h1.shape[1], g.shape[1], keep.shape[1]
    mine = pl.multiple_of(me[0] * w_half, 128)
    other = pl.multiple_of((1 - me[0]) * w_half, 128)

    def copies(k):
        t = step[0] * (CHUNK // UNIT) + k
        src = t
        for s in range(segs - 1):
            first, last = seg_tiles(tab, 0, s)
            src = src + jnp.where(t >= last, all_units // segs - (last - first), 0)
        rows = pl.ds(pl.multiple_of(jnp.minimum(src, all_units - 1) * UNIT, UNIT), UNIT)
        to = pl.ds(pl.multiple_of(k * UNIT, UNIT), UNIT)
        return [
            pltpu.make_async_copy(h1.at[rows, :], out.at[to, pl.ds(0, hid)], sems.at[k, 0]),
            pltpu.make_async_copy(h3.at[rows, :], out.at[to, pl.ds(hid, hid)], sems.at[k, 1]),
            pltpu.make_async_copy(g.at[rows, :], out.at[to, pl.ds(2 * hid, width)], sems.at[k, 2]),
            pltpu.make_async_copy(x.at[rows, pl.ds(other, w_half)], out.at[to, pl.ds(2 * hid + width, w_half)], sems.at[k, 3]),
            pltpu.make_async_copy(x.at[rows, pl.ds(mine, w_half)], keep.at[to, :], sems.at[k, 4]),
        ]

    dx_copy = pltpu.make_async_copy(dx, out.at[:, pl.ds(2 * hid + width + w_half, w_half)], dx_sem)
    dx_copy.start()
    for k in range(CHUNK // UNIT):
        for c in copies(k):
            c.start()
    dx_copy.wait()
    for k in range(CHUNK // UNIT):
        for c in copies(k):
            c.wait()


def pack(tab, me, i, h1, h3, g, x, dx):
    hid, width = h1.shape[1], g.shape[1]
    anywhere = pl.BlockSpec(memory_space=pl.ANY)
    cols = 2 * hid + 2 * width
    return pl.pallas_call(
        pack_kernel,
        grid_spec=pltpu.PrefetchScalarGridSpec(
            num_scalar_prefetch=3,
            grid=(1,),
            in_specs=[anywhere] * 5,
            out_specs=[pl.BlockSpec((CHUNK, cols), lambda *_: (0, 0)), pl.BlockSpec((CHUNK, width // 2), lambda *_: (0, 0))],
            scratch_shapes=[pltpu.SemaphoreType.DMA((CHUNK // UNIT, 5)), pltpu.SemaphoreType.DMA],
        ),
        out_shape=[jax.ShapeDtypeStruct((CHUNK, cols), BF16), jax.ShapeDtypeStruct((CHUNK, width // 2), BF16)],
        compiler_params=pltpu.CompilerParams(vmem_limit_bytes=32 * 1024 * 1024, dimension_semantics=('arbitrary',)),
        cost_estimate=pl.CostEstimate(flops=4 * CHUNK * cols * 256, bytes_accessed=4 * CHUNK * cols, transcendentals=0),
    )(tab, me, i, h1, h3, g, x, dx)


def unpack_kernel(tab, me, mine, back, out, sems):
    segs = tab.shape[1] // 2
    cap, w_half = out.shape[0] // segs, mine.shape[1]
    work = []
    for s in range(segs):
        first, _ = seg_tiles(tab, 0, s)
        rows = pl.ds(pl.multiple_of(2 * CHUNK + first * UNIT, UNIT), cap)
        for k, (buf, half) in enumerate(((mine, me[0]), (back, 1 - me[0]))):
            cols = pl.ds(pl.multiple_of(half * w_half, 128), w_half)
            work.append(pltpu.make_async_copy(buf.at[rows, :], out.at[pl.ds(s * cap, cap), cols], sems.at[s, k]))
    for c in work:
        c.start()
    for c in work:
        c.wait()


def unpack(tab, me, mine, back, slots_n):
    width = 2 * mine.shape[1]
    return pl.pallas_call(
        unpack_kernel,
        grid_spec=pltpu.PrefetchScalarGridSpec(
            num_scalar_prefetch=2,
            grid=(1,),
            in_specs=[pl.BlockSpec(memory_space=pl.ANY)] * 2,
            out_specs=pl.BlockSpec((slots_n, width), lambda *_: (0, 0)),
            scratch_shapes=[pltpu.SemaphoreType.DMA((tab.shape[1] // 2, 2))],
        ),
        out_shape=jax.ShapeDtypeStruct((slots_n, width), BF16),
        compiler_params=pltpu.CompilerParams(vmem_limit_bytes=32 * 1024 * 1024, dimension_semantics=('arbitrary',)),
    )(tab, me, mine, back)


def chunk_kernel(tiles, do_dw, do_dx, tab, me, step, *refs):
    refs = list(refs)
    take = lambda n: [refs.pop(0) for _ in range(n)]
    h1_a, h3_a, g_a, x_a, h1_b, h3_b, g_b, x_b, d_b, w2_a, w2_b, w1, w3 = take(13)
    i1, i2, i3 = take(3) if do_dw else (None,) * 3
    if do_dx:
        take(2)
    o1, o2, o3 = take(3) if do_dw else (None,) * 3
    dx_b, o4, o5, sum_a, sum_b = take(5) if do_dx else (None,) * 5
    e, t = expert_at(tab, step[0], pl.program_id(0)), pl.program_id(1)
    half = tiles // 2
    segs = tab.shape[1] // 2

    if do_dx:
        @pl.when((pl.program_id(0) == 0) & (t == 0))
        def _():
            sum_a[...] = jnp.zeros_like(sum_a)
            sum_b[...] = jnp.zeros_like(sum_b)

    @pl.when(touched(tab, step[0], e))
    def _():
        w2 = jnp.where(t // half == me[0], w2_a[0], w2_b[0])
        row = step[0] * CHUNK + lax.broadcasted_iota(I32, (CHUNK, 1), 0)

        def part(side, h1_ref, h3_ref, g_ref, total):
            here = row < -CHUNK
            for s in range(segs):
                first, _ = seg_tiles(tab, side, s)
                fill = jnp.where(e == s // (segs // 2), tab[side, segs + s], 0)
                here = here | ((row >= first * UNIT) & (row < first * UNIT + fill))
            h1, h3 = h1_ref[...].astype(F32), h3_ref[...].astype(F32)
            sig = jax.nn.sigmoid(h1)
            silu = h1 * sig
            da = jnp.where(here, dot_nt(g_ref[...], w2), 0.0)
            dh1 = (da * h3 * sig * (1.0 + h1 * (1.0 - sig))).astype(BF16)
            dh3 = (da * silu).astype(BF16)
            act = jnp.where(here, silu * h3, 0.0).astype(BF16)
            if do_dx:
                total[...] += dot_nt(dh1, w1[0]) + dot_nt(dh3, w3[0])
            return dh1, dh3, act

        dh1_a, dh3_a, act_a = part(0, h1_a, h3_a, g_a, sum_a)
        dh1_b, dh3_b, act_b = part(1, h1_b, h3_b, g_b, sum_b)
        if do_dw:
            o1[0] = i1[0] + (dot_tn(x_a[...], dh1_a) + dot_tn(x_b[...], dh1_b))
            o3[0] = i3[0] + (dot_tn(x_a[...], dh3_a) + dot_tn(x_b[...], dh3_b))

            @pl.when(t // half == me[0])
            def _():
                o2[0] = i2[0] + (dot_tn(act_a, g_a[...]) + dot_tn(act_b, g_b[...]))

    if do_dx:
        @pl.when((pl.program_id(0) == 1) & (t == tiles - 1))
        def _():
            dx_b[...] = sum_b[...].astype(BF16)
            o4[...] = sum_a[...].astype(BF16)
            o5[...] = d_b[...]


def chunk_grads(tab, me, i, own, keep, got, w2, far_w2, w1, w3, acc, dx_bufs):
    rows, w_half = keep.shape
    e_loc, hid, width = w2.shape[0], 2 * w2.shape[1], w2.shape[2]
    tiles = hid // TILE
    half = tiles // 2

    def where_to(e, t, tab, step):
        e = expert_at(tab, step[0], e)
        on = touched(tab, step[0], e)
        return jnp.where(on, e, 1 - e), jnp.where(on, t, 0)

    def cols_at(first, moves):
        return lambda e, t, tab, me, step: (0, first + (where_to(e, t, tab, step)[1] if moves else 0))

    def w_col(e, t, tab, me, step):
        ee, tt = where_to(e, t, tab, step)
        return ee, 0, tt

    def w_half_row(e, t, tab, me, step):
        ee, tt = where_to(e, t, tab, step)
        return ee, jnp.clip(tt - me[0] * half, 0, half - 1), 0

    def w_far_row(e, t, tab, me, step):
        ee, tt = where_to(e, t, tab, step)
        return ee, jnp.clip(tt - (1 - me[0]) * half, 0, half - 1), 0

    shared = [pl.BlockSpec((rows, TILE), cols_at(0, True)), pl.BlockSpec((rows, TILE), cols_at(tiles, True)), pl.BlockSpec((rows, width), cols_at(2 * hid // width, False))]
    x_own = pl.BlockSpec((rows, w_half), cols_at(0, False))
    x_got = pl.BlockSpec((rows, w_half), cols_at((2 * hid + width) // w_half, False))
    dx_got = pl.BlockSpec((rows, w_half), cols_at((2 * hid + width) // w_half + 1, False))
    dx_at = lambda late: pl.BlockSpec((rows, w_half), lambda e, t, tab, me, step: (jnp.maximum(step[0] + late, 0), 0))
    anywhere = pl.BlockSpec(memory_space=pl.ANY)
    weights = [pl.BlockSpec((1, TILE, width), w_half_row), pl.BlockSpec((1, TILE, width), w_far_row), pl.BlockSpec((1, w_half, TILE), w_col), pl.BlockSpec((1, w_half, TILE), w_col)]
    grads = [pl.BlockSpec((1, w_half, TILE), w_col), pl.BlockSpec((1, TILE, width), w_half_row), pl.BlockSpec((1, w_half, TILE), w_col)]
    do_dw, do_dx = acc is not None, dx_bufs is not None
    given, in_specs, out_specs, out_shape, scratch = [], [], [], [], []
    if do_dw:
        given += acc
        in_specs += grads
        out_specs += grads
        out_shape += [jax.ShapeDtypeStruct(v.shape, F32) for v in acc]
    if do_dx:
        given += dx_bufs
        in_specs += [anywhere, anywhere]
        out_specs += [x_own, dx_at(2), dx_at(0)]
        out_shape += [jax.ShapeDtypeStruct((rows, w_half), BF16)] + [jax.ShapeDtypeStruct(v.shape, BF16) for v in dx_bufs]
        scratch = [pltpu.VMEM((rows, w_half), F32), pltpu.VMEM((rows, w_half), F32)]
    n_dw = 3 if do_dw else 0
    aliases = {16 + k: k for k in range(n_dw)}
    if do_dx:
        aliases.update({16 + n_dw: n_dw + 1, 17 + n_dw: n_dw + 2})
    out = pl.pallas_call(
        functools.partial(chunk_kernel, tiles, do_dw, do_dx),
        grid_spec=pltpu.PrefetchScalarGridSpec(
            num_scalar_prefetch=3,
            grid=(e_loc, tiles),
            in_specs=shared + [x_own] + shared + [x_got, dx_got] + weights + in_specs,
            out_specs=out_specs,
            scratch_shapes=scratch,
        ),
        out_shape=out_shape,
        input_output_aliases=aliases,
        compiler_params=pltpu.CompilerParams(vmem_limit_bytes=56 * 1024 * 1024, dimension_semantics=('arbitrary', 'arbitrary')),
        cost_estimate=pl.CostEstimate(flops=2 * rows * 7 * hid * w_half * 2, bytes_accessed=48 * 1024 * 1024, transcendentals=2 * rows * hid),
    )(tab, me, i, own, own, own, keep, got, got, got, got, got, w2, far_w2, w1, w3, *given)
    return out[n_dw] if do_dx else None, tuple(out[:3]) if do_dw else None, tuple(out[n_dw + 1:]) if do_dx else None


def solution(mesh):
    ep_n = mesh.shape['ep']
    fs_n = mesh.shape['fsdp']
    tok_spec = P(('fsdp', 'ep'), None)
    row_spec = P('ep', 'fsdp', None)
    swap = [(0, 1), (1, 0)]

    def local_backward(grad_out, expert_idx, slot_pos, gates, x_disp, h_gate, h_up, y_disp, w_gate, w_down, w_up):
        tok_n = expert_idx.shape[0]
        e_loc, rows_loc, width = x_disp.shape
        hid = h_gate.shape[2]
        w_half, h_half = width // fs_n, hid // fs_n
        slot_cap = rows_loc // ep_n
        segs = e_loc * ep_n
        slots_n = segs * slot_cap
        me_q = lax.axis_index('fsdp')


        ids, slots = expert_idx[:, 0], slot_pos[:, 0]
        hits = (ids[:, None] == jnp.arange(e_loc * ep_n, dtype=I32)[None, :]) & (slots >= 0)[:, None]
        far_counts = lax.ppermute(jnp.sum(hits.astype(F32), axis=0), 'fsdp', swap)
        far_w_down = lax.ppermute(w_down, 'fsdp', swap)
        send_row = jnp.where(slots >= 0, ((ids % e_loc) * ep_n + ids // e_loc) * slot_cap + slots, slots_n)
        src_choice = jnp.full((slots_n,), tok_n, I32).at[send_row].set(jnp.arange(tok_n, dtype=I32), mode='drop')
        send_dy = jnp.take(grad_out, src_choice, axis=0, mode='fill', fill_value=0).reshape(e_loc, ep_n, slot_cap, width)
        src_choice, send_dy = lax.optimization_barrier((src_choice, send_dy))
        recv_dy = lax.all_to_all(send_dy, 'ep', 1, 1, tiled=True).reshape(slots_n, width)
        send_gate = jnp.take(gates.reshape(-1), src_choice, mode='fill', fill_value=-1).reshape(e_loc, ep_n, slot_cap)
        far_counts = jnp.broadcast_to(far_counts.reshape(ep_n, e_loc).T[:, :, None], (e_loc, ep_n, 128 - slot_cap % 128))
        recv = lax.all_to_all(jnp.concatenate([send_gate, far_counts], axis=2), 'ep', 1, 1, tiled=True).reshape(segs, -1)
        recv_gate, far_counts = recv[:, :slot_cap], recv[:, slot_cap].astype(I32)
        acc = (jnp.zeros((e_loc, w_half, hid), F32), jnp.zeros((e_loc, h_half, width), F32), jnp.zeros((e_loc, w_half, hid), F32))
        dx_mine = jnp.zeros(((slots_n // CHUNK + 3) * CHUNK + slot_cap, w_half), BF16)
        dx_back = jnp.zeros(((slots_n // CHUNK + 3) * CHUNK + slot_cap, w_half), BF16)
        dx_wait = jnp.zeros((CHUNK, w_half), BF16)
        recv_gate, acc, dx_mine, dx_back, dx_wait = lax.optimization_barrier((recv_gate, acc, dx_mine, dx_back, dx_wait))
        dgate_rows = jnp.sum(recv_dy.astype(F32) * y_disp.reshape(slots_n, width).astype(F32), axis=1)
        back_gate = lax.all_to_all(dgate_rows.reshape(e_loc, ep_n, slot_cap), 'ep', 1, 1, tiled=True).reshape(slots_n)

        counts = jnp.sum((recv_gate >= 0).astype(I32), axis=1)
        counts = jnp.stack([counts, far_counts])
        units = jnp.cumsum((counts + UNIT - 1) // UNIT, axis=1)
        tab = jnp.concatenate([units, counts], axis=1)
        chunks = (jnp.max(units[:, segs - 1]) * UNIT + CHUNK - 1) // CHUNK
        me = me_q.astype(I32).reshape(1)
        g_rows = (recv_dy.astype(F32) * recv_gate.reshape(slots_n, 1)).astype(BF16)
        rows = (h_gate.reshape(slots_n, hid), h_up.reshape(slots_n, hid), g_rows, x_disp.reshape(slots_n, width))

        def load(i, dx):
            return pack(tab, me, jnp.asarray(i, I32).reshape(1), *rows, dx)

        def grads(i, own, keep, got, sums):
            return chunk_grads(tab, me, jnp.asarray(i, I32).reshape(1), own, keep, got, w_down, far_w_down, w_gate, w_up, *sums)

        def send(v):
            return lax.ppermute(v, 'fsdp', swap)

        dx_wait, back_gate, acc, dx_mine, dx_back = lax.optimization_barrier((dx_wait, back_gate, acc, dx_mine, dx_back))
        even = load(0, dx_wait)

        def body(k, carry):
            even, odd, got, _, sums = carry
            i = 2 * k
            got_even = send(even[0])
            dx, *sums = grads(i - 1, *odd, got, sums)
            odd = load(i + 1, dx)
            got = send(odd[0])
            dx_wait, *sums = grads(i, *even, got_even, sums)
            return load(i + 2, dx_wait), odd, got, dx_wait, tuple(sums)

        def single(k, carry):
            even, odd, got, _, sums = carry
            got_even = send(even[0])
            dx_wait, *sums = grads(chunks - 2, *odd, got, sums)
            return odd, even, got_even, dx_wait, tuple(sums)

        carry = lax.fori_loop(0, chunks // 2, body, (even, even, even[0], dx_wait, (acc, (dx_mine, dx_back))))
        _, odd, got, dx_wait, sums = lax.fori_loop(0, chunks % 2, single, carry)
        acc, bufs = sums
        dx_peer, _, (dx_mine, dx_back) = grads(chunks - 1, *odd, got, (None, bufs))
        dx_back = lax.dynamic_update_slice(dx_back, send(jnp.concatenate([dx_wait, dx_peer])), (chunks * CHUNK, 0))
        acc = grads(chunks - 1, *odd, got, (acc, None))[1]

        dx_rows = unpack(tab, me, dx_mine, dx_back, slots_n).reshape(e_loc, ep_n, slot_cap, width)
        back_dx = lax.all_to_all(dx_rows, 'ep', 1, 1, tiled=True).reshape(slots_n, width)
        grad_x = jnp.take(back_dx, send_row, axis=0, mode='fill', fill_value=0)
        grad_gates = jnp.take(back_gate, send_row, mode='fill', fill_value=0).reshape(tok_n, 1)
        return (grad_x, grad_gates) + acc

    return jax.shard_map(local_backward, mesh=mesh, in_specs=(tok_spec, tok_spec, tok_spec, tok_spec, row_spec, row_spec, row_spec, row_spec, row_spec, row_spec, row_spec), out_specs=(tok_spec, tok_spec, row_spec, row_spec, row_spec), check_vma=False)
```

time: 1000 us -> 927 us (0.927)
  Pallas kernels: 0 us -> 547 us
  waiting for transfers between devices: 722 us -> 217 us
  matrix products: 144 us -> 0 us
  starting transfers between devices: 18.3 us -> 38.1 us
  between operations: 14.8 us -> 1.61 us
  other arithmetic: 11.2 us -> 22 us
    pallas_call x0 -> x44, Pallas kernels: none -> 547 us  [the longest x22 455 us: chunk_grads(): pl.pallas_call(functools.partial(chunk_kernel, tiles, do_dw, do_dx), grid...]
    reduce_scatter x3 -> x0, waiting for transfers between devices: 522 us -> none  [the longest x1 202 us: local_backward(): lax.psum_scatter(dw_down, 'fsdp', scatter_dimension=1, tiled=True)]
    ppermute x0 -> x23, waiting for transfers between devices: none -> 159 us  [the longest x21 132 us: send(): return lax.ppermute(v, 'fsdp', swap)]
    dot_general x6 -> x0, matrix products: 144 us -> none  [the longest x1 33.1 us: expert_grads(): jnp.einsum('erd,efd->erf', g_rows, w_down, preferred_element_type=jnp.flo...]
    all_gather x3 -> x0, waiting for transfers between devices: 121 us -> none  [the longest x1 95.3 us: local_backward(): full_w_up = lax.all_gather(w_up, 'fsdp', axis=1, tiled=True)]
    ppermute x0 -> x23, starting transfers between devices: none -> 25.1 us  [the longest x21 21.2 us: send(): return lax.ppermute(v, 'fsdp', swap)]
    all_to_all x3 -> x2, waiting for transfers between devices: 76.8 us -> 58.1 us  [the longest x1 42.8 us: local_backward(): lax.all_to_all(send_dy, 'ep', 1, 1, tiled=True).reshape(slots_n, width)]
    unnamed x22 -> x29, local copies, waits for them, and re-layouts: 20.8 us -> 12.4 us
  transfers between devices with their start and end apart: 10 -> 26, of which waited for: 8 -> 12; matrix products, arithmetic and copies ran while one was open for 24% -> 7% of each run, Pallas kernels for 0% -> 58%
where the time goes in v1:
time: 927 us; the launch traced here: 924 us
  Pallas kernels  547 us (59%)
  waiting for transfers between devices  217 us (23%)
  local copies, waits for them, and re-layouts  90.8 us (10%)
  starting transfers between devices  38.1 us (4%)
  other arithmetic  22 us (2%)
    pallas_call x22, Pallas kernels, chunk_grads(): pl.pallas_call(functools.partial(chunk_kernel, tiles, do_dw, do_dx), grid...  455 us
    ppermute x21, waiting for transfers between devices, send(): return lax.ppermute(v, 'fsdp', swap)  132 us
    pallas_call x21, Pallas kernels, pack(): pl.pallas_call(pack_kernel, grid_spec=pltpu.PrefetchScalarGridSpec(num_sc...  88.9 us
    all_to_all x1, waiting for transfers between devices, local_backward(): lax.all_to_all(send_dy, 'ep', 1, 1, tiled=True).reshape(slots_n, width)  42.8 us
    ppermute x1, waiting for transfers between devices, local_backward(): far_w_down = lax.ppermute(w_down, 'fsdp', swap)  27.5 us
    ppermute x21, starting transfers between devices, send(): return lax.ppermute(v, 'fsdp', swap)  21.2 us
  transfers between devices with their start and end apart: 26, of which 12 were waited for; matrix products, arithmetic and copies ran while one was open for 7% of the time, Pallas kernels for 58%

profile of v1, /device:TPU:0, one launch (start us, length us, event | category | flops | bytes accessed | tf_op | source)
XLA Modules:
  0.0 923.9 jit_solution(12514649676902094357)
XLA Ops:
  54.8 42.8 %all-to-all-done.1 = bf16[2,4,320,768]{3,2,0,1:T(8,128)(2,1)} async-done(((bf16[2,4,320,768]{3,2,0,1:T(8,128)(2,1)}), bf16[2,4,320,768]{3,2,0,1:T(8,128)(2,1)}, u32[]{:S(2)}, u32[]{:S(2)}) %all-to-all-start.1) | async-done | bytes 3932192 | tf_op jit(solution)/shard_map/all_to_all | solution.py:279
  129.2 27.5 %collective-permute-done.4.refs_10_ = bf16[2,1536,768]{2,1,0:T(8,128)(2,1)} collective-permute-done((bf16[2,1536,768]{2,1,0:T(8,128)(2,1)}, bf16[2,1536,768]{2,1,0:T(8,128)(2,1)}, u32[]{:S(2)}, u32[]{:S(2)}) %collective-permute-start.4) | collective-permute-done | bytes 4718624 | tf_op jit(solution)/shard_map/ppermute | solution.py:274
  161.0 666.9 %while.64 = (s32[]{:T(128)}, bf16[128,7680]{1,0:T(8,128)(2,1)}, bf16[128,384]{1,0:T(8,128)(2,1)}, bf16[128,7680]{1,0:T(8,128)(2,1)}, bf16[128,384]{1,0:T(8,128)(...) while((s32[]{:T(128)}, bf16[128,7680]{1,0:T(8,128)(2,1)}, ...), condition=%wide.region_7.8_spmd, body=%wide.region_6.7_spmd.sunk | while | flops 10468982784 | bytes 156500448 | solution.py:329
  161.5 21.1 %body.19 = (f32[2,384,3072]{2,1,0:T(8,128)}, f32[2,1536,768]{2,1,0:T(8,128)}, f32[2,384,3072]{2,1,0:T(8,128)}, bf16[128,384]{1,0:T(8,128)(2,1)}, bf16[3264,384]{1,0:T(8,128)(2,1)}, /*index=5*/bf16[3264,384]{1,0:T(8,128)(2,1)}) custom-call(s32[2,16]{1,0:T(2,128)S(1)} %get-tuple-element.1058.tab,, ...), custom_call_target="tpu_custom_call", output_to_operand_aliasing={{0}: (16, {}), {1}: (17, {}), {2}: (18, {}), {4}: (19, {}),... | custom-call | flops 4227858432 | bytes 50331648 | tf_op jit(solution)/shard_map/while/body/pallas_call | solution.py:236
  189.2 17.8 %collective-permute-done.refs_4_.refs_5_.refs_6_.refs_7_.refs_8_ = bf16[128,7680]{1,0:T(8,128)(2,1)} collective-permute-done((bf16[128,7680]{1,0:T(8,128)(2,1)}, bf16[128,7680]{1,0:T(8,128)(2,1)}, u32[]{:S(2)}, u32[]{:S(2)}) %collective-permute-start) | collective-permute-done | bytes 1966112 | tf_op jit(solution)/shard_map/while/body/ppermute | solution.py:308
  207.0 21.4 %body.20 = (f32[2,384,3072]{2,1,0:T(8,128)}, f32[2,1536,768]{2,1,0:T(8,128)}, f32[2,384,3072]{2,1,0:T(8,128)}, bf16[128,384]{1,0:T(8,128)(2,1)S(1)}, bf16[3264,3...) custom-call(s32[2,16]{1,0:T(2,128)S(1)} %get-tuple-element.1058.tab,, ...), custom_call_target="tpu_custom_call", output_to_operand_aliasing={{0}: (16, {}), {1}: (17, {}), {2}: (18, {}), {4}: (19, {}),... | custom-call | flops 4227858432 | bytes 50331648 | tf_op jit(solution)/shard_map/while/body/pallas_call | solution.py:236
  232.7 15.0 %collective-permute-done.1 = bf16[128,7680]{1,0:T(8,128)(2,1)S(1)} collective-permute-done((bf16[128,7680]{1,0:T(8,128)(2,1)}, bf16[128,7680]{1,0:T(8,128)(2,1)S(1)}, u32[]{:S(2)}, u32[]{:S(2)}) %collective-permute-start.1) | collective-permute-done | bytes 1966112 | tf_op jit(solution)/shard_map/while/body/ppermute | solution.py:308
  248.2 21.1 %body.19 = (f32[2,384,3072]{2,1,0:T(8,128)}, f32[2,1536,768]{2,1,0:T(8,128)}, f32[2,384,3072]{2,1,0:T(8,128)}, bf16[128,384]{1,0:T(8,128)(2,1)}, bf16[3264,384]{1,0:T(8,128)(2,1)}, /*index=5*/bf16[3264,384]{1,0:T(8,128)(2,1)}) custom-call(s32[2,16]{1,0:T(2,128)S(1)} %get-tuple-element.1058.tab,, ...), custom_call_target="tpu_custom_call", output_to_operand_aliasing={{0}: (16, {}), {1}: (17, {}), {2}: (18, {}), {4}: (19, {}),... | custom-call | flops 4227858432 | bytes 50331648 | tf_op jit(solution)/shard_map/while/body/pallas_call | solution.py:236
  275.8 17.8 %collective-permute-done.refs_4_.refs_5_.refs_6_.refs_7_.refs_8_ = bf16[128,7680]{1,0:T(8,128)(2,1)} collective-permute-done((bf16[128,7680]{1,0:T(8,128)(2,1)}, bf16[128,7680]{1,0:T(8,128)(2,1)}, u32[]{:S(2)}, u32[]{:S(2)}) %collective-permute-start) | collective-permute-done | bytes 1966112 | tf_op jit(solution)/shard_map/while/body/ppermute | solution.py:308
  293.6 21.4 %body.20 = (f32[2,384,3072]{2,1,0:T(8,128)}, f32[2,1536,768]{2,1,0:T(8,128)}, f32[2,384,3072]{2,1,0:T(8,128)}, bf16[128,384]{1,0:T(8,128)(2,1)S(1)}, bf16[3264,3...) custom-call(s32[2,16]{1,0:T(2,128)S(1)} %get-tuple-element.1058.tab,, ...), custom_call_target="tpu_custom_call", output_to_operand_aliasing={{0}: (16, {}), {1}: (17, {}), {2}: (18, {}), {4}: (19, {}),... | custom-call | flops 4227858432 | bytes 50331648 | tf_op jit(solution)/shard_map/while/body/pallas_call | solution.py:236
  319.3 14.2 %collective-permute-done.1 = bf16[128,7680]{1,0:T(8,128)(2,1)S(1)} collective-permute-done((bf16[128,7680]{1,0:T(8,128)(2,1)}, bf16[128,7680]{1,0:T(8,128)(2,1)S(1)}, u32[]{:S(2)}, u32[]{:S(2)}) %collective-permute-start.1) | collective-permute-done | bytes 1966112 | tf_op jit(solution)/shard_map/while/body/ppermute | solution.py:308
  334.0 21.1 %body.19 = (f32[2,384,3072]{2,1,0:T(8,128)}, f32[2,1536,768]{2,1,0:T(8,128)}, f32[2,384,3072]{2,1,0:T(8,128)}, bf16[128,384]{1,0:T(8,128)(2,1)}, bf16[3264,384]{1,0:T(8,128)(2,1)}, /*index=5*/bf16[3264,384]{1,0:T(8,128)(2,1)}) custom-call(s32[2,16]{1,0:T(2,128)S(1)} %get-tuple-element.1058.tab,, ...), custom_call_target="tpu_custom_call", output_to_operand_aliasing={{0}: (16, {}), {1}: (17, {}), {2}: (18, {}), {4}: (19, {}),... | custom-call | flops 4227858432 | bytes 50331648 | tf_op jit(solution)/shard_map/while/body/pallas_call | solution.py:236
  361.7 17.8 %collective-permute-done.refs_4_.refs_5_.refs_6_.refs_7_.refs_8_ = bf16[128,7680]{1,0:T(8,128)(2,1)} collective-permute-done((bf16[128,7680]{1,0:T(8,128)(2,1)}, bf16[128,7680]{1,0:T(8,128)(2,1)}, u32[]{:S(2)}, u32[]{:S(2)}) %collective-permute-start) | collective-permute-done | bytes 1966112 | tf_op jit(solution)/shard_map/while/body/ppermute | solution.py:308
  379.5 21.4 %body.20 = (f32[2,384,3072]{2,1,0:T(8,128)}, f32[2,1536,768]{2,1,0:T(8,128)}, f32[2,384,3072]{2,1,0:T(8,128)}, bf16[128,384]{1,0:T(8,128)(2,1)S(1)}, bf16[3264,3...) custom-call(s32[2,16]{1,0:T(2,128)S(1)} %get-tuple-element.1058.tab,, ...), custom_call_target="tpu_custom_call", output_to_operand_aliasing={{0}: (16, {}), {1}: (17, {}), {2}: (18, {}), {4}: (19, {}),... | custom-call | flops 4227858432 | bytes 50331648 | tf_op jit(solution)/shard_map/while/body/pallas_call | solution.py:236
  420.2 21.1 %body.19 = (f32[2,384,3072]{2,1,0:T(8,128)}, f32[2,1536,768]{2,1,0:T(8,128)}, f32[2,384,3072]{2,1,0:T(8,128)}, bf16[128,384]{1,0:T(8,128)(2,1)}, bf16[3264,384]{1,0:T(8,128)(2,1)}, /*index=5*/bf16[3264,384]{1,0:T(8,128)(2,1)}) custom-call(s32[2,16]{1,0:T(2,128)S(1)} %get-tuple-element.1058.tab,, ...), custom_call_target="tpu_custom_call", output_to_operand_aliasing={{0}: (16, {}), {1}: (17, {}), {2}: (18, {}), {4}: (19, {}),... | custom-call | flops 4227858432 | bytes 50331648 | tf_op jit(solution)/shard_map/while/body/pallas_call | solution.py:236
  446.7 17.8 %collective-permute-done.refs_4_.refs_5_.refs_6_.refs_7_.refs_8_ = bf16[128,7680]{1,0:T(8,128)(2,1)} collective-permute-done((bf16[128,7680]{1,0:T(8,128)(2,1)}, bf16[128,7680]{1,0:T(8,128)(2,1)}, u32[]{:S(2)}, u32[]{:S(2)}) %collective-permute-start) | collective-permute-done | bytes 1966112 | tf_op jit(solution)/shard_map/while/body/ppermute | solution.py:308
  464.5 21.4 %body.20 = (f32[2,384,3072]{2,1,0:T(8,128)}, f32[2,1536,768]{2,1,0:T(8,128)}, f32[2,384,3072]{2,1,0:T(8,128)}, bf16[128,384]{1,0:T(8,128)(2,1)S(1)}, bf16[3264,3...) custom-call(s32[2,16]{1,0:T(2,128)S(1)} %get-tuple-element.1058.tab,, ...), custom_call_target="tpu_custom_call", output_to_operand_aliasing={{0}: (16, {}), {1}: (17, {}), {2}: (18, {}), {4}: (19, {}),... | custom-call | flops 4227858432 | bytes 50331648 | tf_op jit(solution)/shard_map/while/body/pallas_call | solution.py:236
  490.2 13.7 %collective-permute-done.1 = bf16[128,7680]{1,0:T(8,128)(2,1)S(1)} collective-permute-done((bf16[128,7680]{1,0:T(8,128)(2,1)}, bf16[128,7680]{1,0:T(8,128)(2,1)S(1)}, u32[]{:S(2)}, u32[]{:S(2)}) %collective-permute-start.1) | collective-permute-done | bytes 1966112 | tf_op jit(solution)/shard_map/while/body/ppermute | solution.py:308
  505.6 21.1 %body.19 = (f32[2,384,3072]{2,1,0:T(8,128)}, f32[2,1536,768]{2,1,0:T(8,128)}, f32[2,384,3072]{2,1,0:T(8,128)}, bf16[128,384]{1,0:T(8,128)(2,1)}, bf16[3264,384]{1,0:T(8,128)(2,1)}, /*index=5*/bf16[3264,384]{1,0:T(8,128)(2,1)}) custom-call(s32[2,16]{1,0:T(2,128)S(1)} %get-tuple-element.1058.tab,, ...), custom_call_target="tpu_custom_call", output_to_operand_aliasing={{0}: (16, {}), {1}: (17, {}), {2}: (18, {}), {4}: (19, {}),... | custom-call | flops 4227858432 | bytes 50331648 | tf_op jit(solution)/shard_map/while/body/pallas_call | solution.py:236
  532.0 21.4 %body.20 = (f32[2,384,3072]{2,1,0:T(8,128)}, f32[2,1536,768]{2,1,0:T(8,128)}, f32[2,384,3072]{2,1,0:T(8,128)}, bf16[128,384]{1,0:T(8,128)(2,1)S(1)}, bf16[3264,3...) custom-call(s32[2,16]{1,0:T(2,128)S(1)} %get-tuple-element.1058.tab,, ...), custom_call_target="tpu_custom_call", output_to_operand_aliasing={{0}: (16, {}), {1}: (17, {}), {2}: (18, {}), {4}: (19, {}),... | custom-call | flops 4227858432 | bytes 50331648 | tf_op jit(solution)/shard_map/while/body/pallas_call | solution.py:236
  559.5 21.1 %body.19 = (f32[2,384,3072]{2,1,0:T(8,128)}, f32[2,1536,768]{2,1,0:T(8,128)}, f32[2,384,3072]{2,1,0:T(8,128)}, bf16[128,384]{1,0:T(8,128)(2,1)}, bf16[3264,384]{1,0:T(8,128)(2,1)}, /*index=5*/bf16[3264,384]{1,0:T(8,128)(2,1)}) custom-call(s32[2,16]{1,0:T(2,128)S(1)} %get-tuple-element.1058.tab,, ...), custom_call_target="tpu_custom_call", output_to_operand_aliasing={{0}: (16, {}), {1}: (17, {}), {2}: (18, {}), {4}: (19, {}),... | custom-call | flops 4227858432 | bytes 50331648 | tf_op jit(solution)/shard_map/while/body/pallas_call | solution.py:236
  585.9 21.4 %body.20 = (f32[2,384,3072]{2,1,0:T(8,128)}, f32[2,1536,768]{2,1,0:T(8,128)}, f32[2,384,3072]{2,1,0:T(8,128)}, bf16[128,384]{1,0:T(8,128)(2,1)S(1)}, bf16[3264,3...) custom-call(s32[2,16]{1,0:T(2,128)S(1)} %get-tuple-element.1058.tab,, ...), custom_call_target="tpu_custom_call", output_to_operand_aliasing={{0}: (16, {}), {1}: (17, {}), {2}: (18, {}), {4}: (19, {}),... | custom-call | flops 4227858432 | bytes 50331648 | tf_op jit(solution)/shard_map/while/body/pallas_call | solution.py:236
  613.3 21.1 %body.19 = (f32[2,384,3072]{2,1,0:T(8,128)}, f32[2,1536,768]{2,1,0:T(8,128)}, f32[2,384,3072]{2,1,0:T(8,128)}, bf16[128,384]{1,0:T(8,128)(2,1)}, bf16[3264,384]{1,0:T(8,128)(2,1)}, /*index=5*/bf16[3264,384]{1,0:T(8,128)(2,1)}) custom-call(s32[2,16]{1,0:T(2,128)S(1)} %get-tuple-element.1058.tab,, ...), custom_call_target="tpu_custom_call", output_to_operand_aliasing={{0}: (16, {}), {1}: (17, {}), {2}: (18, {}), {4}: (19, {}),... | custom-call | flops 4227858432 | bytes 50331648 | tf_op jit(solution)/shard_map/while/body/pallas_call | solution.py:236
  639.8 21.4 %body.20 = (f32[2,384,3072]{2,1,0:T(8,128)}, f32[2,1536,768]{2,1,0:T(8,128)}, f32[2,384,3072]{2,1,0:T(8,128)}, bf16[128,384]{1,0:T(8,128)(2,1)S(1)}, bf16[3264,3...) custom-call(s32[2,16]{1,0:T(2,128)S(1)} %get-tuple-element.1058.tab,, ...), custom_call_target="tpu_custom_call", output_to_operand_aliasing={{0}: (16, {}), {1}: (17, {}), {2}: (18, {}), {4}: (19, {}),... | custom-call | flops 4227858432 | bytes 50331648 | tf_op jit(solution)/shard_map/while/body/pallas_call | solution.py:236
  667.2 21.1 %body.19 = (f32[2,384,3072]{2,1,0:T(8,128)}, f32[2,1536,768]{2,1,0:T(8,128)}, f32[2,384,3072]{2,1,0:T(8,128)}, bf16[128,384]{1,0:T(8,128)(2,1)}, bf16[3264,384]{1,0:T(8,128)(2,1)}, /*index=5*/bf16[3264,384]{1,0:T(8,128)(2,1)}) custom-call(s32[2,16]{1,0:T(2,128)S(1)} %get-tuple-element.1058.tab,, ...), custom_call_target="tpu_custom_call", output_to_operand_aliasing={{0}: (16, {}), {1}: (17, {}), {2}: (18, {}), {4}: (19, {}),... | custom-call | flops 4227858432 | bytes 50331648 | tf_op jit(solution)/shard_map/while/body/pallas_call | solution.py:236
  693.7 21.4 %body.20 = (f32[2,384,3072]{2,1,0:T(8,128)}, f32[2,1536,768]{2,1,0:T(8,128)}, f32[2,384,3072]{2,1,0:T(8,128)}, bf16[128,384]{1,0:T(8,128)(2,1)S(1)}, bf16[3264,3...) custom-call(s32[2,16]{1,0:T(2,128)S(1)} %get-tuple-element.1058.tab,, ...), custom_call_target="tpu_custom_call", output_to_operand_aliasing={{0}: (16, {}), {1}: (17, {}), {2}: (18, {}), {4}: (19, {}),... | custom-call | flops 4227858432 | bytes 50331648 | tf_op jit(solution)/shard_map/while/body/pallas_call | solution.py:236
  721.0 21.1 %body.19 = (f32[2,384,3072]{2,1,0:T(8,128)}, f32[2,1536,768]{2,1,0:T(8,128)}, f32[2,384,3072]{2,1,0:T(8,128)}, bf16[128,384]{1,0:T(8,128)(2,1)}, bf16[3264,384]{1,0:T(8,128)(2,1)}, /*index=5*/bf16[3264,384]{1,0:T(8,128)(2,1)}) custom-call(s32[2,16]{1,0:T(2,128)S(1)} %get-tuple-element.1058.tab,, ...), custom_call_target="tpu_custom_call", output_to_operand_aliasing={{0}: (16, {}), {1}: (17, {}), {2}: (18, {}), {4}: (19, {}),... | custom-call | flops 4227858432 | bytes 50331648 | tf_op jit(solution)/shard_map/while/body/pallas_call | solution.py:236
  747.6 21.4 %body.20 = (f32[2,384,3072]{2,1,0:T(8,128)}, f32[2,1536,768]{2,1,0:T(8,128)}, f32[2,384,3072]{2,1,0:T(8,128)}, bf16[128,384]{1,0:T(8,128)(2,1)S(1)}, bf16[3264,3...) custom-call(s32[2,16]{1,0:T(2,128)S(1)} %get-tuple-element.1058.tab,, ...), custom_call_target="tpu_custom_call", output_to_operand_aliasing={{0}: (16, {}), {1}: (17, {}), {2}: (18, {}), {4}: (19, {}),... | custom-call | flops 4227858432 | bytes 50331648 | tf_op jit(solution)/shard_map/while/body/pallas_call | solution.py:236
  774.8 21.1 %body.19 = (f32[2,384,3072]{2,1,0:T(8,128)}, f32[2,1536,768]{2,1,0:T(8,128)}, f32[2,384,3072]{2,1,0:T(8,128)}, bf16[128,384]{1,0:T(8,128)(2,1)}, bf16[3264,384]{1,0:T(8,128)(2,1)}, /*index=5*/bf16[3264,384]{1,0:T(8,128)(2,1)}) custom-call(s32[2,16]{1,0:T(2,128)S(1)} %get-tuple-element.1058.tab,, ...), custom_call_target="tpu_custom_call", output_to_operand_aliasing={{0}: (16, {}), {1}: (17, {}), {2}: (18, {}), {4}: (19, {}),... | custom-call | flops 4227858432 | bytes 50331648 | tf_op jit(solution)/shard_map/while/body/pallas_call | solution.py:236
  801.5 21.4 %body.20 = (f32[2,384,3072]{2,1,0:T(8,128)}, f32[2,1536,768]{2,1,0:T(8,128)}, f32[2,384,3072]{2,1,0:T(8,128)}, bf16[128,384]{1,0:T(8,128)(2,1)S(1)}, bf16[3264,3...) custom-call(s32[2,16]{1,0:T(2,128)S(1)} %get-tuple-element.1058.tab,, ...), custom_call_target="tpu_custom_call", output_to_operand_aliasing={{0}: (16, {}), {1}: (17, {}), {2}: (18, {}), {4}: (19, {}),... | custom-call | flops 4227858432 | bytes 50331648 | tf_op jit(solution)/shard_map/while/body/pallas_call | solution.py:236
  870.6 17.6 %shard_map.149 = (f32[2,384,3072]{2,1,0:T(8,128)}, f32[2,1536,768]{2,1,0:T(8,128)}, f32[2,384,3072]{2,1,0:T(8,128)}) custom-call(s32[2,16]{1,0:T(2,128)S(1)} %get-tuple-element.1148, s32[1]{0:T(128)} %bitcast.11.me, s32[1]{0:T(128)} %bitcast.12.step, ...), custom_call_target="tpu_custom_call", output_to_operand_aliasing={{0}: (16, {}), {1}: (17, {}), {2}: (18, {})} | custom-call | flops 4227858432 | bytes 50331648 | tf_op jit(solution)/shard_map/pallas_call | solution.py:236
  888.2 15.3 %all-to-all-done.3 = bf16[2,4,320,768]{3,2,0,1:T(8,128)(2,1)} async-done(((bf16[2,4,320,768]{3,2,0,1:T(8,128)(2,1)}), bf16[2,4,320,768]{3,2,0,1:T(8,128)(2,1)}, u32[]{:S(2)}, u32[]{:S(2)}) %all-to-all-start.3) | async-done | bytes 3932192 | tf_op jit(solution)/shard_map/all_to_all | solution.py:337
  (225 shorter events, 279.4 us)
Async XLA Ops:
  3.0 37.6 %collective-permute-start.3 = (f32[8]{0:T(128)S(1)}, f32[8]{0:T(128)S(1)}, u32[]{:S(2)}, u32[]{:S(2)}) collective-permute-start(f32[8]{0:T(128)S(1)} %convert_reduce_fusion), channel_id=1, source_target_pairs={{0,4},{4,0},{1,5},{5,1},{2,6},{6,2},{3,7},{7,3}} | collective-permute-start | bytes 104 | tf_op jit(solution)/shard_map/ppermute | solution.py:273
  47.4 50.2 %all-to-all-start.1 = ((bf16[2,4,320,768]{3,2,0,1:T(8,128)(2,1)}), bf16[2,4,320,768]{3,2,0,1:T(8,128)(2,1)}, u32[]{:S(2)}, u32[]{:S(2)}) async-start(bf16[2,4,320,768]{3,2,0,1:T(8,128)(2,1)} %copy_select_fusion), calls=%async_computation.1 | async-start | bytes 7864320 | tf_op jit(solution)/shard_map/all_to_all | solution.py:279
  52.2 104.5 %collective-permute-start.4 = (bf16[2,1536,768]{2,1,0:T(8,128)(2,1)}, bf16[2,1536,768]{2,1,0:T(8,128)(2,1)}, u32[]{:S(2)}, u32[]{:S(2)}) collective-permute-start(bf16[2,1536,768]{2,1,0:T(8,128)(2,1)} %refs_9_.3), channel_id=1, source_target_pairs={{0,4},{4,0},{1,5},{5,1},{2,6},{6,2},{3,7},{7,3}} | collective-permute-start | bytes 14155784 | tf_op jit(solution)/shard_map/ppermute | solution.py:274
  102.6 8.5 all-to-all-start.2
  161.0 46.0 %collective-permute-start = (bf16[128,7680]{1,0:T(8,128)(2,1)}, bf16[128,7680]{1,0:T(8,128)(2,1)}, u32[]{:S(2)}, u32[]{:S(2)}) collective-permute-start(bf16[128,7680]{1,0:T(8,128)(2,1)} %get-tuple-element.1020.refs_0_.refs_1_.refs_2_), channel_id=1, source_target_pairs={{0,4},{4,0},{1,5},{5,1},{2,6},{6,2},{3,7},{7,3}} | collective-permute-start | bytes 5898248 | tf_op jit(solution)/shard_map/while/body/ppermute | solution.py:308
  187.8 59.9 %collective-permute-start.1 = (bf16[128,7680]{1,0:T(8,128)(2,1)}, bf16[128,7680]{1,0:T(8,128)(2,1)S(1)}, u32[]{:S(2)}, u32[]{:S(2)}) collective-permute-start(bf16[128,7680]{1,0:T(8,128)(2,1)} %get-tuple-element.1048), channel_id=1, source_target_pairs={{0,4},{4,0},{1,5},{5,1},{2,6},{6,2},{3,7},{7,3}} | collective-permute-start | bytes 5898248 | tf_op jit(solution)/shard_map/while/body/ppermute | solution.py:308
  207.0 21.4 %copy-start.11 = (bf16[2560,768]{1,0:T(8,128)(2,1)S(1)}, bf16[2560,768]{1,0:T(8,128)(2,1)}, u32[]{:S(2)}) copy-start(bf16[2560,768]{1,0:T(8,128)(2,1)} %get-tuple-element.1066.g) | copy-start | bytes 11796484 | tf_op jit(solution)/shard_map/while
  247.7 45.9 %collective-permute-start = (bf16[128,7680]{1,0:T(8,128)(2,1)}, bf16[128,7680]{1,0:T(8,128)(2,1)}, u32[]{:S(2)}, u32[]{:S(2)}) collective-permute-start(bf16[128,7680]{1,0:T(8,128)(2,1)} %get-tuple-element.1020.refs_0_.refs_1_.refs_2_), channel_id=1, source_target_pairs={{0,4},{4,0},{1,5},{5,1},{2,6},{6,2},{3,7},{7,3}} | collective-permute-start | bytes 5898248 | tf_op jit(solution)/shard_map/while/body/ppermute | solution.py:308
  274.4 59.1 %collective-permute-start.1 = (bf16[128,7680]{1,0:T(8,128)(2,1)}, bf16[128,7680]{1,0:T(8,128)(2,1)S(1)}, u32[]{:S(2)}, u32[]{:S(2)}) collective-permute-start(bf16[128,7680]{1,0:T(8,128)(2,1)} %get-tuple-element.1048), channel_id=1, source_target_pairs={{0,4},{4,0},{1,5},{5,1},{2,6},{6,2},{3,7},{7,3}} | collective-permute-start | bytes 5898248 | tf_op jit(solution)/shard_map/while/body/ppermute | solution.py:308
  293.6 21.4 %copy-start.11 = (bf16[2560,768]{1,0:T(8,128)(2,1)S(1)}, bf16[2560,768]{1,0:T(8,128)(2,1)}, u32[]{:S(2)}) copy-start(bf16[2560,768]{1,0:T(8,128)(2,1)} %get-tuple-element.1066.g) | copy-start | bytes 11796484 | tf_op jit(solution)/shard_map/while
  333.5 46.0 %collective-permute-start = (bf16[128,7680]{1,0:T(8,128)(2,1)}, bf16[128,7680]{1,0:T(8,128)(2,1)}, u32[]{:S(2)}, u32[]{:S(2)}) collective-permute-start(bf16[128,7680]{1,0:T(8,128)(2,1)} %get-tuple-element.1020.refs_0_.refs_1_.refs_2_), channel_id=1, source_target_pairs={{0,4},{4,0},{1,5},{5,1},{2,6},{6,2},{3,7},{7,3}} | collective-permute-start | bytes 5898248 | tf_op jit(solution)/shard_map/while/body/ppermute | solution.py:308
  360.2 58.3 %collective-permute-start.1 = (bf16[128,7680]{1,0:T(8,128)(2,1)}, bf16[128,7680]{1,0:T(8,128)(2,1)S(1)}, u32[]{:S(2)}, u32[]{:S(2)}) collective-permute-start(bf16[128,7680]{1,0:T(8,128)(2,1)} %get-tuple-element.1048), channel_id=1, source_target_pairs={{0,4},{4,0},{1,5},{5,1},{2,6},{6,2},{3,7},{7,3}} | collective-permute-start | bytes 5898248 | tf_op jit(solution)/shard_map/while/body/ppermute | solution.py:308
  379.5 21.4 %copy-start.11 = (bf16[2560,768]{1,0:T(8,128)(2,1)S(1)}, bf16[2560,768]{1,0:T(8,128)(2,1)}, u32[]{:S(2)}) copy-start(bf16[2560,768]{1,0:T(8,128)(2,1)} %get-tuple-element.1066.g) | copy-start | bytes 11796484 | tf_op jit(solution)/shard_map/while
  418.5 46.0 %collective-permute-start = (bf16[128,7680]{1,0:T(8,128)(2,1)}, bf16[128,7680]{1,0:T(8,128)(2,1)}, u32[]{:S(2)}, u32[]{:S(2)}) collective-permute-start(bf16[128,7680]{1,0:T(8,128)(2,1)} %get-tuple-element.1020.refs_0_.refs_1_.refs_2_), channel_id=1, source_target_pairs={{0,4},{4,0},{1,5},{5,1},{2,6},{6,2},{3,7},{7,3}} | collective-permute-start | bytes 5898248 | tf_op jit(solution)/shard_map/while/body/ppermute | solution.py:308
  446.4 57.4 %collective-permute-start.1 = (bf16[128,7680]{1,0:T(8,128)(2,1)}, bf16[128,7680]{1,0:T(8,128)(2,1)S(1)}, u32[]{:S(2)}, u32[]{:S(2)}) collective-permute-start(bf16[128,7680]{1,0:T(8,128)(2,1)} %get-tuple-element.1048), channel_id=1, source_target_pairs={{0,4},{4,0},{1,5},{5,1},{2,6},{6,2},{3,7},{7,3}} | collective-permute-start | bytes 5898248 | tf_op jit(solution)/shard_map/while/body/ppermute | solution.py:308
  503.9 28.2 %collective-permute-start = (bf16[128,7680]{1,0:T(8,128)(2,1)}, bf16[128,7680]{1,0:T(8,128)(2,1)}, u32[]{:S(2)}, u32[]{:S(2)}) collective-permute-start(bf16[128,7680]{1,0:T(8,128)(2,1)} %get-tuple-element.1020.refs_0_.refs_1_.refs_2_), channel_id=1, source_target_pairs={{0,4},{4,0},{1,5},{5,1},{2,6},{6,2},{3,7},{7,3}} | collective-permute-start | bytes 5898248 | tf_op jit(solution)/shard_map/while/body/ppermute | solution.py:308
  531.8 25.9 %collective-permute-start.1 = (bf16[128,7680]{1,0:T(8,128)(2,1)}, bf16[128,7680]{1,0:T(8,128)(2,1)S(1)}, u32[]{:S(2)}, u32[]{:S(2)}) collective-permute-start(bf16[128,7680]{1,0:T(8,128)(2,1)} %get-tuple-element.1048), channel_id=1, source_target_pairs={{0,4},{4,0},{1,5},{5,1},{2,6},{6,2},{3,7},{7,3}} | collective-permute-start | bytes 5898248 | tf_op jit(solution)/shard_map/while/body/ppermute | solution.py:308
  557.7 28.2 %collective-permute-start = (bf16[128,7680]{1,0:T(8,128)(2,1)}, bf16[128,7680]{1,0:T(8,128)(2,1)}, u32[]{:S(2)}, u32[]{:S(2)}) collective-permute-start(bf16[128,7680]{1,0:T(8,128)(2,1)} %get-tuple-element.1020.refs_0_.refs_1_.refs_2_), channel_id=1, source_target_pairs={{0,4},{4,0},{1,5},{5,1},{2,6},{6,2},{3,7},{7,3}} | collective-permute-start | bytes 5898248 | tf_op jit(solution)/shard_map/while/body/ppermute | solution.py:308
  585.7 25.9 %collective-permute-start.1 = (bf16[128,7680]{1,0:T(8,128)(2,1)}, bf16[128,7680]{1,0:T(8,128)(2,1)S(1)}, u32[]{:S(2)}, u32[]{:S(2)}) collective-permute-start(bf16[128,7680]{1,0:T(8,128)(2,1)} %get-tuple-element.1048), channel_id=1, source_target_pairs={{0,4},{4,0},{1,5},{5,1},{2,6},{6,2},{3,7},{7,3}} | collective-permute-start | bytes 5898248 | tf_op jit(solution)/shard_map/while/body/ppermute | solution.py:308
  611.6 28.2 %collective-permute-start = (bf16[128,7680]{1,0:T(8,128)(2,1)}, bf16[128,7680]{1,0:T(8,128)(2,1)}, u32[]{:S(2)}, u32[]{:S(2)}) collective-permute-start(bf16[128,7680]{1,0:T(8,128)(2,1)} %get-tuple-element.1020.refs_0_.refs_1_.refs_2_), channel_id=1, source_target_pairs={{0,4},{4,0},{1,5},{5,1},{2,6},{6,2},{3,7},{7,3}} | collective-permute-start | bytes 5898248 | tf_op jit(solution)/shard_map/while/body/ppermute | solution.py:308
  639.5 26.0 %collective-permute-start.1 = (bf16[128,7680]{1,0:T(8,128)(2,1)}, bf16[128,7680]{1,0:T(8,128)(2,1)S(1)}, u32[]{:S(2)}, u32[]{:S(2)}) collective-permute-start(bf16[128,7680]{1,0:T(8,128)(2,1)} %get-tuple-element.1048), channel_id=1, source_target_pairs={{0,4},{4,0},{1,5},{5,1},{2,6},{6,2},{3,7},{7,3}} | collective-permute-start | bytes 5898248 | tf_op jit(solution)/shard_map/while/body/ppermute | solution.py:308
  665.5 28.2 %collective-permute-start = (bf16[128,7680]{1,0:T(8,128)(2,1)}, bf16[128,7680]{1,0:T(8,128)(2,1)}, u32[]{:S(2)}, u32[]{:S(2)}) collective-permute-start(bf16[128,7680]{1,0:T(8,128)(2,1)} %get-tuple-element.1020.refs_0_.refs_1_.refs_2_), channel_id=1, source_target_pairs={{0,4},{4,0},{1,5},{5,1},{2,6},{6,2},{3,7},{7,3}} | collective-permute-start | bytes 5898248 | tf_op jit(solution)/shard_map/while/body/ppermute | solution.py:308
  693.4 26.0 %collective-permute-start.1 = (bf16[128,7680]{1,0:T(8,128)(2,1)}, bf16[128,7680]{1,0:T(8,128)(2,1)S(1)}, u32[]{:S(2)}, u32[]{:S(2)}) collective-permute-start(bf16[128,7680]{1,0:T(8,128)(2,1)} %get-tuple-element.1048), channel_id=1, source_target_pairs={{0,4},{4,0},{1,5},{5,1},{2,6},{6,2},{3,7},{7,3}} | collective-permute-start | bytes 5898248 | tf_op jit(solution)/shard_map/while/body/ppermute | solution.py:308
  693.7 21.4 %copy-start.11 = (bf16[2560,768]{1,0:T(8,128)(2,1)S(1)}, bf16[2560,768]{1,0:T(8,128)(2,1)}, u32[]{:S(2)}) copy-start(bf16[2560,768]{1,0:T(8,128)(2,1)} %get-tuple-element.1066.g) | copy-start | bytes 11796484 | tf_op jit(solution)/shard_map/while
  719.4 28.2 %collective-permute-start = (bf16[128,7680]{1,0:T(8,128)(2,1)}, bf16[128,7680]{1,0:T(8,128)(2,1)}, u32[]{:S(2)}, u32[]{:S(2)}) collective-permute-start(bf16[128,7680]{1,0:T(8,128)(2,1)} %get-tuple-element.1020.refs_0_.refs_1_.refs_2_), channel_id=1, source_target_pairs={{0,4},{4,0},{1,5},{5,1},{2,6},{6,2},{3,7},{7,3}} | collective-permute-start | bytes 5898248 | tf_op jit(solution)/shard_map/while/body/ppermute | solution.py:308
  747.2 26.1 %collective-permute-start.1 = (bf16[128,7680]{1,0:T(8,128)(2,1)}, bf16[128,7680]{1,0:T(8,128)(2,1)S(1)}, u32[]{:S(2)}, u32[]{:S(2)}) collective-permute-start(bf16[128,7680]{1,0:T(8,128)(2,1)} %get-tuple-element.1048), channel_id=1, source_target_pairs={{0,4},{4,0},{1,5},{5,1},{2,6},{6,2},{3,7},{7,3}} | collective-permute-start | bytes 5898248 | tf_op jit(solution)/shard_map/while/body/ppermute | solution.py:308
  747.6 21.4 %copy-start.11 = (bf16[2560,768]{1,0:T(8,128)(2,1)S(1)}, bf16[2560,768]{1,0:T(8,128)(2,1)}, u32[]{:S(2)}) copy-start(bf16[2560,768]{1,0:T(8,128)(2,1)} %get-tuple-element.1066.g) | copy-start | bytes 11796484 | tf_op jit(solution)/shard_map/while
  773.3 28.2 %collective-permute-start = (bf16[128,7680]{1,0:T(8,128)(2,1)}, bf16[128,7680]{1,0:T(8,128)(2,1)}, u32[]{:S(2)}, u32[]{:S(2)}) collective-permute-start(bf16[128,7680]{1,0:T(8,128)(2,1)} %get-tuple-element.1020.refs_0_.refs_1_.refs_2_), channel_id=1, source_target_pairs={{0,4},{4,0},{1,5},{5,1},{2,6},{6,2},{3,7},{7,3}} | collective-permute-start | bytes 5898248 | tf_op jit(solution)/shard_map/while/body/ppermute | solution.py:308
  801.1 26.8 %collective-permute-start.1 = (bf16[128,7680]{1,0:T(8,128)(2,1)}, bf16[128,7680]{1,0:T(8,128)(2,1)S(1)}, u32[]{:S(2)}, u32[]{:S(2)}) collective-permute-start(bf16[128,7680]{1,0:T(8,128)(2,1)} %get-tuple-element.1048), channel_id=1, source_target_pairs={{0,4},{4,0},{1,5},{5,1},{2,6},{6,2},{3,7},{7,3}} | collective-permute-start | bytes 5898248 | tf_op jit(solution)/shard_map/while/body/ppermute | solution.py:308
  801.5 21.4 %copy-start.11 = (bf16[2560,768]{1,0:T(8,128)(2,1)S(1)}, bf16[2560,768]{1,0:T(8,128)(2,1)}, u32[]{:S(2)}) copy-start(bf16[2560,768]{1,0:T(8,128)(2,1)} %get-tuple-element.1066.g) | copy-start | bytes 11796484 | tf_op jit(solution)/shard_map/while
  841.7 5.7 collective-permute-start.5
  853.2 50.4 %all-to-all-start.3 = ((bf16[2,4,320,768]{3,2,0,1:T(8,128)(2,1)}), bf16[2,4,320,768]{3,2,0,1:T(8,128)(2,1)}, u32[]{:S(2)}, u32[]{:S(2)}) async-start(bf16[2,4,320,768]{3,2,0,1:T(8,128)(2,1)} %copy.73), calls=%async_computation.3 | async-start | bytes 7864320 | tf_op jit(solution)/shard_map/all_to_all | solution.py:337
  (46 other events, 452.9 us)

commit v2 on v1

--- a/solution.py
+++ b/solution.py
@@ -31,7 +31,7 @@
     lo, hi = i * (CHUNK // UNIT), (i + 1) * (CHUNK // UNIT)
     one = ((tab[0, segs // 2 - 1] < hi) & (tab[0, segs - 1] > lo)) | ((tab[1, segs // 2 - 1] < hi) & (tab[1, segs - 1] > lo))
     zero = (tab[0, segs // 2 - 1] > lo) | (tab[1, segs // 2 - 1] > lo) | jnp.logical_not(one)
-    return jnp.where(e == 0, zero, one)
+    return jnp.where(e == 0, zero, one) | (i < 0)
 
 
 def expert_at(tab, i, turn):
@@ -167,12 +167,12 @@
         dh1_a, dh3_a, act_a = part(0, h1_a, h3_a, g_a, sum_a)
         dh1_b, dh3_b, act_b = part(1, h1_b, h3_b, g_b, sum_b)
         if do_dw:
-            o1[0] = i1[0] + (dot_tn(x_a[...], dh1_a) + dot_tn(x_b[...], dh1_b))
-            o3[0] = i3[0] + (dot_tn(x_a[...], dh3_a) + dot_tn(x_b[...], dh3_b))
+            o1[0] = jnp.where(step[0] < 0, 0.0, i1[0] + (dot_tn(x_a[...], dh1_a) + dot_tn(x_b[...], dh1_b)))
+            o3[0] = jnp.where(step[0] < 0, 0.0, i3[0] + (dot_tn(x_a[...], dh3_a) + dot_tn(x_b[...], dh3_b)))
 
             @pl.when(t // half == me[0])
             def _():
-                o2[0] = i2[0] + (dot_tn(act_a, g_a[...]) + dot_tn(act_b, g_b[...]))
+                o2[0] = jnp.where(step[0] < 0, 0.0, i2[0] + (dot_tn(act_a, g_a[...]) + dot_tn(act_b, g_b[...])))
 
     if do_dx:
         @pl.when((pl.program_id(0) == 1) & (t == tiles - 1))
@@ -250,6 +250,10 @@
     return out[n_dw] if do_dx else None, tuple(out[:3]) if do_dw else None, tuple(out[n_dw + 1:]) if do_dx else None
 
 
+def room(shapes):
+    return tuple(pl.pallas_call(lambda *refs: None, out_shape=[jax.ShapeDtypeStruct(v, F32) for v in shapes], out_specs=[pl.BlockSpec(memory_space=pl.ANY)] * len(shapes))())
+
+
 def solution(mesh):
     ep_n = mesh.shape['ep']
     fs_n = mesh.shape['fsdp']
@@ -281,7 +285,7 @@
         far_counts = jnp.broadcast_to(far_counts.reshape(ep_n, e_loc).T[:, :, None], (e_loc, ep_n, 128 - slot_cap % 128))
         recv = lax.all_to_all(jnp.concatenate([send_gate, far_counts], axis=2), 'ep', 1, 1, tiled=True).reshape(segs, -1)
         recv_gate, far_counts = recv[:, :slot_cap], recv[:, slot_cap].astype(I32)
-        acc = (jnp.zeros((e_loc, w_half, hid), F32), jnp.zeros((e_loc, h_half, width), F32), jnp.zeros((e_loc, w_half, hid), F32))
+        acc = room([(e_loc, w_half, hid), (e_loc, h_half, width), (e_loc, w_half, hid)])
         dx_mine = jnp.zeros(((slots_n // CHUNK + 3) * CHUNK + slot_cap, w_half), BF16)
         dx_back = jnp.zeros(((slots_n // CHUNK + 3) * CHUNK + slot_cap, w_half), BF16)
         dx_wait = jnp.zeros((CHUNK, w_half), BF16)

time: 927 us -> 924 us (level)
  Pallas kernels: 547 us -> 562 us
  local copies, waits for them, and re-layouts: 90.8 us -> 77.3 us
    pallas_call x22, Pallas kernels: 455 us -> 470 us  [chunk_grads(): pl.pallas_call(functools.partial(chunk_kernel, tiles, do_dw, do_dx), grid...]
    ppermute x21, waiting for transfers between devices: 132 us -> 117 us  [send(): return lax.ppermute(v, 'fsdp', swap)]
  transfers between devices with their start and end apart: 26 -> 26, of which waited for: 12 -> 12; matrix products, arithmetic and copies ran while one was open for 7% -> 7% of each run, Pallas kernels for 58% -> 59%
where the time goes in v2:
time: 924 us; the launch traced here: 921 us
  Pallas kernels  562 us (61%)
  waiting for transfers between devices  212 us (23%)
  local copies, waits for them, and re-layouts  77.3 us (8%)
  starting transfers between devices  38.2 us (4%)
  other arithmetic  22 us (2%)
    pallas_call x22, Pallas kernels, chunk_grads(): pl.pallas_call(functools.partial(chunk_kernel, tiles, do_dw, do_dx), grid...  470 us
    ppermute x21, waiting for transfers between devices, send(): return lax.ppermute(v, 'fsdp', swap)  117 us
    pallas_call x21, Pallas kernels, pack(): pl.pallas_call(pack_kernel, grid_spec=pltpu.PrefetchScalarGridSpec(num_sc...  88.9 us
    all_to_all x1, waiting for transfers between devices, local_backward(): lax.all_to_all(send_dy, 'ep', 1, 1, tiled=True).reshape(slots_n, width)  42.8 us
    ppermute x1, waiting for transfers between devices, local_backward(): far_w_down = lax.ppermute(w_down, 'fsdp', swap)  36.6 us
    ppermute x21, starting transfers between devices, send(): return lax.ppermute(v, 'fsdp', swap)  21.3 us
  transfers between devices with their start and end apart: 26, of which 12 were waited for; matrix products, arithmetic and copies ran while one was open for 7% of the time, Pallas kernels for 59%

profile of v2, /device:TPU:0, one launch (start us, length us, event | category | flops | bytes accessed | tf_op | source)
XLA Modules:
  0.0 920.6 jit_solution(427013051379612353)
XLA Ops:
  26.9 13.6 %gather_fusion.1 = f32[2560]{0:T(1024)S(1)} fusion(f32[2048]{0:T(1024)S(1)} %bitcast.39, s32[3072]{0:T(1024)S(1)} %pad_clamp_fusion), kind=kCustom, calls=%fused_computation.1 | custom fusion | bytes 30720 | tf_op jit(solution)/shard_map/jit(_take)/gather | solution.py:284
  54.8 42.8 %all-to-all-done.1 = bf16[2,4,320,768]{3,2,0,1:T(8,128)(2,1)} async-done(((bf16[2,4,320,768]{3,2,0,1:T(8,128)(2,1)}), bf16[2,4,320,768]{3,2,0,1:T(8,128)(2,1)}, u32[]{:S(2)}, u32[]{:S(2)}) %all-to-all-start.1) | async-done | bytes 3932192 | tf_op jit(solution)/shard_map/all_to_all | solution.py:283
  120.0 36.6 %collective-permute-done.4.refs_10_ = bf16[2,1536,768]{2,1,0:T(8,128)(2,1)} collective-permute-done((bf16[2,1536,768]{2,1,0:T(8,128)(2,1)}, bf16[2,1536,768]{2,1,0:T(8,128)(2,1)}, u32[]{:S(2)}, u32[]{:S(2)}) %collective-permute-start.4) | collective-permute-done | bytes 4718624 | tf_op jit(solution)/shard_map/ppermute | solution.py:278
  156.6 668.0 %while.64 = (s32[]{:T(128)}, bf16[128,7680]{1,0:T(8,128)(2,1)}, bf16[128,384]{1,0:T(8,128)(2,1)}, bf16[128,7680]{1,0:T(8,128)(2,1)}, bf16[128,384]{1,0:T(8,128)(...) while((s32[]{:T(128)}, bf16[128,7680]{1,0:T(8,128)(2,1)}, ...), condition=%wide.region_7.8_spmd, body=%wide.region_6.7_spmd.sunk | while | flops 10468982784 | bytes 156500448 | solution.py:333
  157.2 34.7 %body.19 = (f32[2,384,3072]{2,1,0:T(8,128)}, f32[2,1536,768]{2,1,0:T(8,128)}, f32[2,384,3072]{2,1,0:T(8,128)}, bf16[128,384]{1,0:T(8,128)(2,1)}, bf16[3264,384]{1,0:T(8,128)(2,1)}, /*index=5*/bf16[3264,384]{1,0:T(8,128)(2,1)}) custom-call(s32[2,16]{1,0:T(2,128)S(1)} %get-tuple-element.1064.tab,, ...), custom_call_target="tpu_custom_call", output_to_operand_aliasing={{0}: (16, {}), {1}: (17, {}), {2}: (18, {}), {4}: (19, {}),... | custom-call | flops 4227858432 | bytes 50331648 | tf_op jit(solution)/shard_map/while/body/pallas_call | solution.py:236
  202.7 21.4 %body.20 = (f32[2,384,3072]{2,1,0:T(8,128)}, f32[2,1536,768]{2,1,0:T(8,128)}, f32[2,384,3072]{2,1,0:T(8,128)}, bf16[128,384]{1,0:T(8,128)(2,1)S(1)}, bf16[3264,3...) custom-call(s32[2,16]{1,0:T(2,128)S(1)} %get-tuple-element.1064.tab,, ...), custom_call_target="tpu_custom_call", output_to_operand_aliasing={{0}: (16, {}), {1}: (17, {}), {2}: (18, {}), {4}: (19, {}),... | custom-call | flops 4227858432 | bytes 50331648 | tf_op jit(solution)/shard_map/while/body/pallas_call | solution.py:236
  228.4 14.9 %collective-permute-done.1 = bf16[128,7680]{1,0:T(8,128)(2,1)S(1)} collective-permute-done((bf16[128,7680]{1,0:T(8,128)(2,1)}, bf16[128,7680]{1,0:T(8,128)(2,1)S(1)}, u32[]{:S(2)}, u32[]{:S(2)}) %collective-permute-start.1) | collective-permute-done | bytes 1966112 | tf_op jit(solution)/shard_map/while/body/ppermute | solution.py:312
  243.8 21.2 %body.19 = (f32[2,384,3072]{2,1,0:T(8,128)}, f32[2,1536,768]{2,1,0:T(8,128)}, f32[2,384,3072]{2,1,0:T(8,128)}, bf16[128,384]{1,0:T(8,128)(2,1)}, bf16[3264,384]{1,0:T(8,128)(2,1)}, /*index=5*/bf16[3264,384]{1,0:T(8,128)(2,1)}) custom-call(s32[2,16]{1,0:T(2,128)S(1)} %get-tuple-element.1064.tab,, ...), custom_call_target="tpu_custom_call", output_to_operand_aliasing={{0}: (16, {}), {1}: (17, {}), {2}: (18, {}), {4}: (19, {}),... | custom-call | flops 4227858432 | bytes 50331648 | tf_op jit(solution)/shard_map/while/body/pallas_call | solution.py:236
  271.6 17.1 %collective-permute-done.refs_4_.refs_5_.refs_6_.refs_7_.refs_8_ = bf16[128,7680]{1,0:T(8,128)(2,1)} collective-permute-done((bf16[128,7680]{1,0:T(8,128)(2,1)}, bf16[128,7680]{1,0:T(8,128)(2,1)}, u32[]{:S(2)}, u32[]{:S(2)}) %collective-permute-start) | collective-permute-done | bytes 1966112 | tf_op jit(solution)/shard_map/while/body/ppermute | solution.py:312
  288.7 21.4 %body.20 = (f32[2,384,3072]{2,1,0:T(8,128)}, f32[2,1536,768]{2,1,0:T(8,128)}, f32[2,384,3072]{2,1,0:T(8,128)}, bf16[128,384]{1,0:T(8,128)(2,1)S(1)}, bf16[3264,3...) custom-call(s32[2,16]{1,0:T(2,128)S(1)} %get-tuple-element.1064.tab,, ...), custom_call_target="tpu_custom_call", output_to_operand_aliasing={{0}: (16, {}), {1}: (17, {}), {2}: (18, {}), {4}: (19, {}),... | custom-call | flops 4227858432 | bytes 50331648 | tf_op jit(solution)/shard_map/while/body/pallas_call | solution.py:236
  314.5 14.6 %collective-permute-done.1 = bf16[128,7680]{1,0:T(8,128)(2,1)S(1)} collective-permute-done((bf16[128,7680]{1,0:T(8,128)(2,1)}, bf16[128,7680]{1,0:T(8,128)(2,1)S(1)}, u32[]{:S(2)}, u32[]{:S(2)}) %collective-permute-start.1) | collective-permute-done | bytes 1966112 | tf_op jit(solution)/shard_map/while/body/ppermute | solution.py:312
  330.1 21.2 %body.19 = (f32[2,384,3072]{2,1,0:T(8,128)}, f32[2,1536,768]{2,1,0:T(8,128)}, f32[2,384,3072]{2,1,0:T(8,128)}, bf16[128,384]{1,0:T(8,128)(2,1)}, bf16[3264,384]{1,0:T(8,128)(2,1)}, /*index=5*/bf16[3264,384]{1,0:T(8,128)(2,1)}) custom-call(s32[2,16]{1,0:T(2,128)S(1)} %get-tuple-element.1064.tab,, ...), custom_call_target="tpu_custom_call", output_to_operand_aliasing={{0}: (16, {}), {1}: (17, {}), {2}: (18, {}), {4}: (19, {}),... | custom-call | flops 4227858432 | bytes 50331648 | tf_op jit(solution)/shard_map/while/body/pallas_call | solution.py:236
  357.4 17.7 %collective-permute-done.refs_4_.refs_5_.refs_6_.refs_7_.refs_8_ = bf16[128,7680]{1,0:T(8,128)(2,1)} collective-permute-done((bf16[128,7680]{1,0:T(8,128)(2,1)}, bf16[128,7680]{1,0:T(8,128)(2,1)}, u32[]{:S(2)}, u32[]{:S(2)}) %collective-permute-start) | collective-permute-done | bytes 1966112 | tf_op jit(solution)/shard_map/while/body/ppermute | solution.py:312
  375.1 21.4 %body.20 = (f32[2,384,3072]{2,1,0:T(8,128)}, f32[2,1536,768]{2,1,0:T(8,128)}, f32[2,384,3072]{2,1,0:T(8,128)}, bf16[128,384]{1,0:T(8,128)(2,1)S(1)}, bf16[3264,3...) custom-call(s32[2,16]{1,0:T(2,128)S(1)} %get-tuple-element.1064.tab,, ...), custom_call_target="tpu_custom_call", output_to_operand_aliasing={{0}: (16, {}), {1}: (17, {}), {2}: (18, {}), {4}: (19, {}),... | custom-call | flops 4227858432 | bytes 50331648 | tf_op jit(solution)/shard_map/while/body/pallas_call | solution.py:236
  400.9 13.8 %collective-permute-done.1 = bf16[128,7680]{1,0:T(8,128)(2,1)S(1)} collective-permute-done((bf16[128,7680]{1,0:T(8,128)(2,1)}, bf16[128,7680]{1,0:T(8,128)(2,1)S(1)}, u32[]{:S(2)}, u32[]{:S(2)}) %collective-permute-start.1) | collective-permute-done | bytes 1966112 | tf_op jit(solution)/shard_map/while/body/ppermute | solution.py:312
  415.9 21.2 %body.19 = (f32[2,384,3072]{2,1,0:T(8,128)}, f32[2,1536,768]{2,1,0:T(8,128)}, f32[2,384,3072]{2,1,0:T(8,128)}, bf16[128,384]{1,0:T(8,128)(2,1)}, bf16[3264,384]{1,0:T(8,128)(2,1)}, /*index=5*/bf16[3264,384]{1,0:T(8,128)(2,1)}) custom-call(s32[2,16]{1,0:T(2,128)S(1)} %get-tuple-element.1064.tab,, ...), custom_call_target="tpu_custom_call", output_to_operand_aliasing={{0}: (16, {}), {1}: (17, {}), {2}: (18, {}), {4}: (19, {}),... | custom-call | flops 4227858432 | bytes 50331648 | tf_op jit(solution)/shard_map/while/body/pallas_call | solution.py:236
  442.9 17.7 %collective-permute-done.refs_4_.refs_5_.refs_6_.refs_7_.refs_8_ = bf16[128,7680]{1,0:T(8,128)(2,1)} collective-permute-done((bf16[128,7680]{1,0:T(8,128)(2,1)}, bf16[128,7680]{1,0:T(8,128)(2,1)}, u32[]{:S(2)}, u32[]{:S(2)}) %collective-permute-start) | collective-permute-done | bytes 1966112 | tf_op jit(solution)/shard_map/while/body/ppermute | solution.py:312
  460.6 21.4 %body.20 = (f32[2,384,3072]{2,1,0:T(8,128)}, f32[2,1536,768]{2,1,0:T(8,128)}, f32[2,384,3072]{2,1,0:T(8,128)}, bf16[128,384]{1,0:T(8,128)(2,1)S(1)}, bf16[3264,3...) custom-call(s32[2,16]{1,0:T(2,128)S(1)} %get-tuple-element.1064.tab,, ...), custom_call_target="tpu_custom_call", output_to_operand_aliasing={{0}: (16, {}), {1}: (17, {}), {2}: (18, {}), {4}: (19, {}),... | custom-call | flops 4227858432 | bytes 50331648 | tf_op jit(solution)/shard_map/while/body/pallas_call | solution.py:236
  500.8 21.2 %body.19 = (f32[2,384,3072]{2,1,0:T(8,128)}, f32[2,1536,768]{2,1,0:T(8,128)}, f32[2,384,3072]{2,1,0:T(8,128)}, bf16[128,384]{1,0:T(8,128)(2,1)}, bf16[3264,384]{1,0:T(8,128)(2,1)}, /*index=5*/bf16[3264,384]{1,0:T(8,128)(2,1)}) custom-call(s32[2,16]{1,0:T(2,128)S(1)} %get-tuple-element.1064.tab,, ...), custom_call_target="tpu_custom_call", output_to_operand_aliasing={{0}: (16, {}), {1}: (17, {}), {2}: (18, {}), {4}: (19, {}),... | custom-call | flops 4227858432 | bytes 50331648 | tf_op jit(solution)/shard_map/while/body/pallas_call | solution.py:236
  527.6 21.4 %body.20 = (f32[2,384,3072]{2,1,0:T(8,128)}, f32[2,1536,768]{2,1,0:T(8,128)}, f32[2,384,3072]{2,1,0:T(8,128)}, bf16[128,384]{1,0:T(8,128)(2,1)S(1)}, bf16[3264,3...) custom-call(s32[2,16]{1,0:T(2,128)S(1)} %get-tuple-element.1064.tab,, ...), custom_call_target="tpu_custom_call", output_to_operand_aliasing={{0}: (16, {}), {1}: (17, {}), {2}: (18, {}), {4}: (19, {}),... | custom-call | flops 4227858432 | bytes 50331648 | tf_op jit(solution)/shard_map/while/body/pallas_call | solution.py:236
  554.8 21.2 %body.19 = (f32[2,384,3072]{2,1,0:T(8,128)}, f32[2,1536,768]{2,1,0:T(8,128)}, f32[2,384,3072]{2,1,0:T(8,128)}, bf16[128,384]{1,0:T(8,128)(2,1)}, bf16[3264,384]{1,0:T(8,128)(2,1)}, /*index=5*/bf16[3264,384]{1,0:T(8,128)(2,1)}) custom-call(s32[2,16]{1,0:T(2,128)S(1)} %get-tuple-element.1064.tab,, ...), custom_call_target="tpu_custom_call", output_to_operand_aliasing={{0}: (16, {}), {1}: (17, {}), {2}: (18, {}), {4}: (19, {}),... | custom-call | flops 4227858432 | bytes 50331648 | tf_op jit(solution)/shard_map/while/body/pallas_call | solution.py:236
  581.7 21.4 %body.20 = (f32[2,384,3072]{2,1,0:T(8,128)}, f32[2,1536,768]{2,1,0:T(8,128)}, f32[2,384,3072]{2,1,0:T(8,128)}, bf16[128,384]{1,0:T(8,128)(2,1)S(1)}, bf16[3264,3...) custom-call(s32[2,16]{1,0:T(2,128)S(1)} %get-tuple-element.1064.tab,, ...), custom_call_target="tpu_custom_call", output_to_operand_aliasing={{0}: (16, {}), {1}: (17, {}), {2}: (18, {}), {4}: (19, {}),... | custom-call | flops 4227858432 | bytes 50331648 | tf_op jit(solution)/shard_map/while/body/pallas_call | solution.py:236
  608.8 21.2 %body.19 = (f32[2,384,3072]{2,1,0:T(8,128)}, f32[2,1536,768]{2,1,0:T(8,128)}, f32[2,384,3072]{2,1,0:T(8,128)}, bf16[128,384]{1,0:T(8,128)(2,1)}, bf16[3264,384]{1,0:T(8,128)(2,1)}, /*index=5*/bf16[3264,384]{1,0:T(8,128)(2,1)}) custom-call(s32[2,16]{1,0:T(2,128)S(1)} %get-tuple-element.1064.tab,, ...), custom_call_target="tpu_custom_call", output_to_operand_aliasing={{0}: (16, {}), {1}: (17, {}), {2}: (18, {}), {4}: (19, {}),... | custom-call | flops 4227858432 | bytes 50331648 | tf_op jit(solution)/shard_map/while/body/pallas_call | solution.py:236
  635.8 21.4 %body.20 = (f32[2,384,3072]{2,1,0:T(8,128)}, f32[2,1536,768]{2,1,0:T(8,128)}, f32[2,384,3072]{2,1,0:T(8,128)}, bf16[128,384]{1,0:T(8,128)(2,1)S(1)}, bf16[3264,3...) custom-call(s32[2,16]{1,0:T(2,128)S(1)} %get-tuple-element.1064.tab,, ...), custom_call_target="tpu_custom_call", output_to_operand_aliasing={{0}: (16, {}), {1}: (17, {}), {2}: (18, {}), {4}: (19, {}),... | custom-call | flops 4227858432 | bytes 50331648 | tf_op jit(solution)/shard_map/while/body/pallas_call | solution.py:236
  662.8 21.2 %body.19 = (f32[2,384,3072]{2,1,0:T(8,128)}, f32[2,1536,768]{2,1,0:T(8,128)}, f32[2,384,3072]{2,1,0:T(8,128)}, bf16[128,384]{1,0:T(8,128)(2,1)}, bf16[3264,384]{1,0:T(8,128)(2,1)}, /*index=5*/bf16[3264,384]{1,0:T(8,128)(2,1)}) custom-call(s32[2,16]{1,0:T(2,128)S(1)} %get-tuple-element.1064.tab,, ...), custom_call_target="tpu_custom_call", output_to_operand_aliasing={{0}: (16, {}), {1}: (17, {}), {2}: (18, {}), {4}: (19, {}),... | custom-call | flops 4227858432 | bytes 50331648 | tf_op jit(solution)/shard_map/while/body/pallas_call | solution.py:236
  689.9 21.4 %body.20 = (f32[2,384,3072]{2,1,0:T(8,128)}, f32[2,1536,768]{2,1,0:T(8,128)}, f32[2,384,3072]{2,1,0:T(8,128)}, bf16[128,384]{1,0:T(8,128)(2,1)S(1)}, bf16[3264,3...) custom-call(s32[2,16]{1,0:T(2,128)S(1)} %get-tuple-element.1064.tab,, ...), custom_call_target="tpu_custom_call", output_to_operand_aliasing={{0}: (16, {}), {1}: (17, {}), {2}: (18, {}), {4}: (19, {}),... | custom-call | flops 4227858432 | bytes 50331648 | tf_op jit(solution)/shard_map/while/body/pallas_call | solution.py:236
  716.8 21.2 %body.19 = (f32[2,384,3072]{2,1,0:T(8,128)}, f32[2,1536,768]{2,1,0:T(8,128)}, f32[2,384,3072]{2,1,0:T(8,128)}, bf16[128,384]{1,0:T(8,128)(2,1)}, bf16[3264,384]{1,0:T(8,128)(2,1)}, /*index=5*/bf16[3264,384]{1,0:T(8,128)(2,1)}) custom-call(s32[2,16]{1,0:T(2,128)S(1)} %get-tuple-element.1064.tab,, ...), custom_call_target="tpu_custom_call", output_to_operand_aliasing={{0}: (16, {}), {1}: (17, {}), {2}: (18, {}), {4}: (19, {}),... | custom-call | flops 4227858432 | bytes 50331648 | tf_op jit(solution)/shard_map/while/body/pallas_call | solution.py:236
  744.0 21.4 %body.20 = (f32[2,384,3072]{2,1,0:T(8,128)}, f32[2,1536,768]{2,1,0:T(8,128)}, f32[2,384,3072]{2,1,0:T(8,128)}, bf16[128,384]{1,0:T(8,128)(2,1)S(1)}, bf16[3264,3...) custom-call(s32[2,16]{1,0:T(2,128)S(1)} %get-tuple-element.1064.tab,, ...), custom_call_target="tpu_custom_call", output_to_operand_aliasing={{0}: (16, {}), {1}: (17, {}), {2}: (18, {}), {4}: (19, {}),... | custom-call | flops 4227858432 | bytes 50331648 | tf_op jit(solution)/shard_map/while/body/pallas_call | solution.py:236
  770.8 21.2 %body.19 = (f32[2,384,3072]{2,1,0:T(8,128)}, f32[2,1536,768]{2,1,0:T(8,128)}, f32[2,384,3072]{2,1,0:T(8,128)}, bf16[128,384]{1,0:T(8,128)(2,1)}, bf16[3264,384]{1,0:T(8,128)(2,1)}, /*index=5*/bf16[3264,384]{1,0:T(8,128)(2,1)}) custom-call(s32[2,16]{1,0:T(2,128)S(1)} %get-tuple-element.1064.tab,, ...), custom_call_target="tpu_custom_call", output_to_operand_aliasing={{0}: (16, {}), {1}: (17, {}), {2}: (18, {}), {4}: (19, {}),... | custom-call | flops 4227858432 | bytes 50331648 | tf_op jit(solution)/shard_map/while/body/pallas_call | solution.py:236
  798.1 21.4 %body.20 = (f32[2,384,3072]{2,1,0:T(8,128)}, f32[2,1536,768]{2,1,0:T(8,128)}, f32[2,384,3072]{2,1,0:T(8,128)}, bf16[128,384]{1,0:T(8,128)(2,1)S(1)}, bf16[3264,3...) custom-call(s32[2,16]{1,0:T(2,128)S(1)} %get-tuple-element.1064.tab,, ...), custom_call_target="tpu_custom_call", output_to_operand_aliasing={{0}: (16, {}), {1}: (17, {}), {2}: (18, {}), {4}: (19, {}),... | custom-call | flops 4227858432 | bytes 50331648 | tf_op jit(solution)/shard_map/while/body/pallas_call | solution.py:236
  867.3 17.7 %shard_map.150 = (f32[2,384,3072]{2,1,0:T(8,128)}, f32[2,1536,768]{2,1,0:T(8,128)}, f32[2,384,3072]{2,1,0:T(8,128)}) custom-call(s32[2,16]{1,0:T(2,128)S(1)} %get-tuple-element.1154, s32[1]{0:T(128)} %bitcast.11.me, s32[1]{0:T(128)} %bitcast.12.step, ...), custom_call_target="tpu_custom_call", output_to_operand_aliasing={{0}: (16, {}), {1}: (17, {}), {2}: (18, {})} | custom-call | flops 4227858432 | bytes 50331648 | tf_op jit(solution)/shard_map/pallas_call | solution.py:236
  885.0 15.3 %all-to-all-done.3 = bf16[2,4,320,768]{3,2,0,1:T(8,128)(2,1)} async-done(((bf16[2,4,320,768]{3,2,0,1:T(8,128)(2,1)}), bf16[2,4,320,768]{3,2,0,1:T(8,128)(2,1)}, u32[]{:S(2)}, u32[]{:S(2)}) %all-to-all-start.3) | async-done | bytes 3932192 | tf_op jit(solution)/shard_map/all_to_all | solution.py:341
  (221 shorter events, 256.7 us)
Async XLA Ops:
  3.0 37.5 %collective-permute-start.3 = (f32[8]{0:T(128)S(1)}, f32[8]{0:T(128)S(1)}, u32[]{:S(2)}, u32[]{:S(2)}) collective-permute-start(f32[8]{0:T(128)S(1)} %convert_reduce_fusion), channel_id=1, source_target_pairs={{0,4},{4,0},{1,5},{5,1},{2,6},{6,2},{3,7},{7,3}} | collective-permute-start | bytes 104 | tf_op jit(solution)/shard_map/ppermute | solution.py:277
  47.3 50.2 %all-to-all-start.1 = ((bf16[2,4,320,768]{3,2,0,1:T(8,128)(2,1)}), bf16[2,4,320,768]{3,2,0,1:T(8,128)(2,1)}, u32[]{:S(2)}, u32[]{:S(2)}) async-start(bf16[2,4,320,768]{3,2,0,1:T(8,128)(2,1)} %copy_select_fusion), calls=%async_computation.1 | async-start | bytes 7864320 | tf_op jit(solution)/shard_map/all_to_all | solution.py:283
  52.2 104.5 %collective-permute-start.4 = (bf16[2,1536,768]{2,1,0:T(8,128)(2,1)}, bf16[2,1536,768]{2,1,0:T(8,128)(2,1)}, u32[]{:S(2)}, u32[]{:S(2)}) collective-permute-start(bf16[2,1536,768]{2,1,0:T(8,128)(2,1)} %refs_9_.3), channel_id=1, source_target_pairs={{0,4},{4,0},{1,5},{5,1},{2,6},{6,2},{3,7},{7,3}} | collective-permute-start | bytes 14155784 | tf_op jit(solution)/shard_map/ppermute | solution.py:278
  102.6 8.5 all-to-all-start.2
  118.4 38.2 %copy-start.6 = (bf16[3264,384]{1,0:T(8,128)(2,1)}, bf16[3264,384]{1,0:T(8,128)(2,1)S(1)}, u32[]{:S(2)}) copy-start(bf16[3264,384]{1,0:T(8,128)(2,1)S(1)} %broadcast.90) | copy-start | bytes 7520260
  156.6 46.0 %collective-permute-start = (bf16[128,7680]{1,0:T(8,128)(2,1)}, bf16[128,7680]{1,0:T(8,128)(2,1)}, u32[]{:S(2)}, u32[]{:S(2)}) collective-permute-start(bf16[128,7680]{1,0:T(8,128)(2,1)} %get-tuple-element.1026.refs_0_.refs_1_.refs_2_), channel_id=1, source_target_pairs={{0,4},{4,0},{1,5},{5,1},{2,6},{6,2},{3,7},{7,3}} | collective-permute-start | bytes 5898248 | tf_op jit(solution)/shard_map/while/body/ppermute | solution.py:312
  157.2 34.7 %copy-start.9 = (bf16[2560,768]{1,0:T(8,128)(2,1)S(1)}, bf16[2560,768]{1,0:T(8,128)(2,1)}, u32[]{:S(2)}) copy-start(bf16[2560,768]{1,0:T(8,128)(2,1)} %get-tuple-element.1072.g) | copy-start | bytes 11796484 | tf_op jit(solution)/shard_map/while
  196.9 46.4 %collective-permute-start.1 = (bf16[128,7680]{1,0:T(8,128)(2,1)}, bf16[128,7680]{1,0:T(8,128)(2,1)S(1)}, u32[]{:S(2)}, u32[]{:S(2)}) collective-permute-start(bf16[128,7680]{1,0:T(8,128)(2,1)} %get-tuple-element.1054), channel_id=1, source_target_pairs={{0,4},{4,0},{1,5},{5,1},{2,6},{6,2},{3,7},{7,3}} | collective-permute-start | bytes 5898248 | tf_op jit(solution)/shard_map/while/body/ppermute | solution.py:312
  202.7 21.5 %copy-start.10 = (bf16[2560,768]{1,0:T(8,128)(2,1)S(1)}, bf16[2560,768]{1,0:T(8,128)(2,1)}, u32[]{:S(2)}) copy-start(bf16[2560,768]{1,0:T(8,128)(2,1)} %get-tuple-element.1072.g) | copy-start | bytes 11796484 | tf_op jit(solution)/shard_map/while
  243.3 45.4 %collective-permute-start = (bf16[128,7680]{1,0:T(8,128)(2,1)}, bf16[128,7680]{1,0:T(8,128)(2,1)}, u32[]{:S(2)}, u32[]{:S(2)}) collective-permute-start(bf16[128,7680]{1,0:T(8,128)(2,1)} %get-tuple-element.1026.refs_0_.refs_1_.refs_2_), channel_id=1, source_target_pairs={{0,4},{4,0},{1,5},{5,1},{2,6},{6,2},{3,7},{7,3}} | collective-permute-start | bytes 5898248 | tf_op jit(solution)/shard_map/while/body/ppermute | solution.py:312
  270.1 59.0 %collective-permute-start.1 = (bf16[128,7680]{1,0:T(8,128)(2,1)}, bf16[128,7680]{1,0:T(8,128)(2,1)S(1)}, u32[]{:S(2)}, u32[]{:S(2)}) collective-permute-start(bf16[128,7680]{1,0:T(8,128)(2,1)} %get-tuple-element.1054), channel_id=1, source_target_pairs={{0,4},{4,0},{1,5},{5,1},{2,6},{6,2},{3,7},{7,3}} | collective-permute-start | bytes 5898248 | tf_op jit(solution)/shard_map/while/body/ppermute | solution.py:312
  329.1 46.0 %collective-permute-start = (bf16[128,7680]{1,0:T(8,128)(2,1)}, bf16[128,7680]{1,0:T(8,128)(2,1)}, u32[]{:S(2)}, u32[]{:S(2)}) collective-permute-start(bf16[128,7680]{1,0:T(8,128)(2,1)} %get-tuple-element.1026.refs_0_.refs_1_.refs_2_), channel_id=1, source_target_pairs={{0,4},{4,0},{1,5},{5,1},{2,6},{6,2},{3,7},{7,3}} | collective-permute-start | bytes 5898248 | tf_op jit(solution)/shard_map/while/body/ppermute | solution.py:312
  356.4 58.2 %collective-permute-start.1 = (bf16[128,7680]{1,0:T(8,128)(2,1)}, bf16[128,7680]{1,0:T(8,128)(2,1)S(1)}, u32[]{:S(2)}, u32[]{:S(2)}) collective-permute-start(bf16[128,7680]{1,0:T(8,128)(2,1)} %get-tuple-element.1054), channel_id=1, source_target_pairs={{0,4},{4,0},{1,5},{5,1},{2,6},{6,2},{3,7},{7,3}} | collective-permute-start | bytes 5898248 | tf_op jit(solution)/shard_map/while/body/ppermute | solution.py:312
  375.1 21.5 %copy-start.10 = (bf16[2560,768]{1,0:T(8,128)(2,1)S(1)}, bf16[2560,768]{1,0:T(8,128)(2,1)}, u32[]{:S(2)}) copy-start(bf16[2560,768]{1,0:T(8,128)(2,1)} %get-tuple-element.1072.g) | copy-start | bytes 11796484 | tf_op jit(solution)/shard_map/while
  414.6 46.0 %collective-permute-start = (bf16[128,7680]{1,0:T(8,128)(2,1)}, bf16[128,7680]{1,0:T(8,128)(2,1)}, u32[]{:S(2)}, u32[]{:S(2)}) collective-permute-start(bf16[128,7680]{1,0:T(8,128)(2,1)} %get-tuple-element.1026.refs_0_.refs_1_.refs_2_), channel_id=1, source_target_pairs={{0,4},{4,0},{1,5},{5,1},{2,6},{6,2},{3,7},{7,3}} | collective-permute-start | bytes 5898248 | tf_op jit(solution)/shard_map/while/body/ppermute | solution.py:312
  442.2 57.1 %collective-permute-start.1 = (bf16[128,7680]{1,0:T(8,128)(2,1)}, bf16[128,7680]{1,0:T(8,128)(2,1)S(1)}, u32[]{:S(2)}, u32[]{:S(2)}) collective-permute-start(bf16[128,7680]{1,0:T(8,128)(2,1)} %get-tuple-element.1054), channel_id=1, source_target_pairs={{0,4},{4,0},{1,5},{5,1},{2,6},{6,2},{3,7},{7,3}} | collective-permute-start | bytes 5898248 | tf_op jit(solution)/shard_map/while/body/ppermute | solution.py:312
  499.3 28.3 %collective-permute-start = (bf16[128,7680]{1,0:T(8,128)(2,1)}, bf16[128,7680]{1,0:T(8,128)(2,1)}, u32[]{:S(2)}, u32[]{:S(2)}) collective-permute-start(bf16[128,7680]{1,0:T(8,128)(2,1)} %get-tuple-element.1026.refs_0_.refs_1_.refs_2_), channel_id=1, source_target_pairs={{0,4},{4,0},{1,5},{5,1},{2,6},{6,2},{3,7},{7,3}} | collective-permute-start | bytes 5898248 | tf_op jit(solution)/shard_map/while/body/ppermute | solution.py:312
  527.1 26.2 %collective-permute-start.1 = (bf16[128,7680]{1,0:T(8,128)(2,1)}, bf16[128,7680]{1,0:T(8,128)(2,1)S(1)}, u32[]{:S(2)}, u32[]{:S(2)}) collective-permute-start(bf16[128,7680]{1,0:T(8,128)(2,1)} %get-tuple-element.1054), channel_id=1, source_target_pairs={{0,4},{4,0},{1,5},{5,1},{2,6},{6,2},{3,7},{7,3}} | collective-permute-start | bytes 5898248 | tf_op jit(solution)/shard_map/while/body/ppermute | solution.py:312
  553.4 28.3 %collective-permute-start = (bf16[128,7680]{1,0:T(8,128)(2,1)}, bf16[128,7680]{1,0:T(8,128)(2,1)}, u32[]{:S(2)}, u32[]{:S(2)}) collective-permute-start(bf16[128,7680]{1,0:T(8,128)(2,1)} %get-tuple-element.1026.refs_0_.refs_1_.refs_2_), channel_id=1, source_target_pairs={{0,4},{4,0},{1,5},{5,1},{2,6},{6,2},{3,7},{7,3}} | collective-permute-start | bytes 5898248 | tf_op jit(solution)/shard_map/while/body/ppermute | solution.py:312
  581.1 26.3 %collective-permute-start.1 = (bf16[128,7680]{1,0:T(8,128)(2,1)}, bf16[128,7680]{1,0:T(8,128)(2,1)S(1)}, u32[]{:S(2)}, u32[]{:S(2)}) collective-permute-start(bf16[128,7680]{1,0:T(8,128)(2,1)} %get-tuple-element.1054), channel_id=1, source_target_pairs={{0,4},{4,0},{1,5},{5,1},{2,6},{6,2},{3,7},{7,3}} | collective-permute-start | bytes 5898248 | tf_op jit(solution)/shard_map/while/body/ppermute | solution.py:312
  607.5 28.3 %collective-permute-start = (bf16[128,7680]{1,0:T(8,128)(2,1)}, bf16[128,7680]{1,0:T(8,128)(2,1)}, u32[]{:S(2)}, u32[]{:S(2)}) collective-permute-start(bf16[128,7680]{1,0:T(8,128)(2,1)} %get-tuple-element.1026.refs_0_.refs_1_.refs_2_), channel_id=1, source_target_pairs={{0,4},{4,0},{1,5},{5,1},{2,6},{6,2},{3,7},{7,3}} | collective-permute-start | bytes 5898248 | tf_op jit(solution)/shard_map/while/body/ppermute | solution.py:312
  635.1 26.4 %collective-permute-start.1 = (bf16[128,7680]{1,0:T(8,128)(2,1)}, bf16[128,7680]{1,0:T(8,128)(2,1)S(1)}, u32[]{:S(2)}, u32[]{:S(2)}) collective-permute-start(bf16[128,7680]{1,0:T(8,128)(2,1)} %get-tuple-element.1054), channel_id=1, source_target_pairs={{0,4},{4,0},{1,5},{5,1},{2,6},{6,2},{3,7},{7,3}} | collective-permute-start | bytes 5898248 | tf_op jit(solution)/shard_map/while/body/ppermute | solution.py:312
  661.6 28.3 %collective-permute-start = (bf16[128,7680]{1,0:T(8,128)(2,1)}, bf16[128,7680]{1,0:T(8,128)(2,1)}, u32[]{:S(2)}, u32[]{:S(2)}) collective-permute-start(bf16[128,7680]{1,0:T(8,128)(2,1)} %get-tuple-element.1026.refs_0_.refs_1_.refs_2_), channel_id=1, source_target_pairs={{0,4},{4,0},{1,5},{5,1},{2,6},{6,2},{3,7},{7,3}} | collective-permute-start | bytes 5898248 | tf_op jit(solution)/shard_map/while/body/ppermute | solution.py:312
  689.1 26.5 %collective-permute-start.1 = (bf16[128,7680]{1,0:T(8,128)(2,1)}, bf16[128,7680]{1,0:T(8,128)(2,1)S(1)}, u32[]{:S(2)}, u32[]{:S(2)}) collective-permute-start(bf16[128,7680]{1,0:T(8,128)(2,1)} %get-tuple-element.1054), channel_id=1, source_target_pairs={{0,4},{4,0},{1,5},{5,1},{2,6},{6,2},{3,7},{7,3}} | collective-permute-start | bytes 5898248 | tf_op jit(solution)/shard_map/while/body/ppermute | solution.py:312
  715.7 28.3 %collective-permute-start = (bf16[128,7680]{1,0:T(8,128)(2,1)}, bf16[128,7680]{1,0:T(8,128)(2,1)}, u32[]{:S(2)}, u32[]{:S(2)}) collective-permute-start(bf16[128,7680]{1,0:T(8,128)(2,1)} %get-tuple-element.1026.refs_0_.refs_1_.refs_2_), channel_id=1, source_target_pairs={{0,4},{4,0},{1,5},{5,1},{2,6},{6,2},{3,7},{7,3}} | collective-permute-start | bytes 5898248 | tf_op jit(solution)/shard_map/while/body/ppermute | solution.py:312
  743.1 26.6 %collective-permute-start.1 = (bf16[128,7680]{1,0:T(8,128)(2,1)}, bf16[128,7680]{1,0:T(8,128)(2,1)S(1)}, u32[]{:S(2)}, u32[]{:S(2)}) collective-permute-start(bf16[128,7680]{1,0:T(8,128)(2,1)} %get-tuple-element.1054), channel_id=1, source_target_pairs={{0,4},{4,0},{1,5},{5,1},{2,6},{6,2},{3,7},{7,3}} | collective-permute-start | bytes 5898248 | tf_op jit(solution)/shard_map/while/body/ppermute | solution.py:312
  744.0 21.5 %copy-start.10 = (bf16[2560,768]{1,0:T(8,128)(2,1)S(1)}, bf16[2560,768]{1,0:T(8,128)(2,1)}, u32[]{:S(2)}) copy-start(bf16[2560,768]{1,0:T(8,128)(2,1)} %get-tuple-element.1072.g) | copy-start | bytes 11796484 | tf_op jit(solution)/shard_map/while
  769.8 28.3 %collective-permute-start = (bf16[128,7680]{1,0:T(8,128)(2,1)}, bf16[128,7680]{1,0:T(8,128)(2,1)}, u32[]{:S(2)}, u32[]{:S(2)}) collective-permute-start(bf16[128,7680]{1,0:T(8,128)(2,1)} %get-tuple-element.1026.refs_0_.refs_1_.refs_2_), channel_id=1, source_target_pairs={{0,4},{4,0},{1,5},{5,1},{2,6},{6,2},{3,7},{7,3}} | collective-permute-start | bytes 5898248 | tf_op jit(solution)/shard_map/while/body/ppermute | solution.py:312
  797.1 27.5 %collective-permute-start.1 = (bf16[128,7680]{1,0:T(8,128)(2,1)}, bf16[128,7680]{1,0:T(8,128)(2,1)S(1)}, u32[]{:S(2)}, u32[]{:S(2)}) collective-permute-start(bf16[128,7680]{1,0:T(8,128)(2,1)} %get-tuple-element.1054), channel_id=1, source_target_pairs={{0,4},{4,0},{1,5},{5,1},{2,6},{6,2},{3,7},{7,3}} | collective-permute-start | bytes 5898248 | tf_op jit(solution)/shard_map/while/body/ppermute | solution.py:312
  798.1 21.5 %copy-start.10 = (bf16[2560,768]{1,0:T(8,128)(2,1)S(1)}, bf16[2560,768]{1,0:T(8,128)(2,1)}, u32[]{:S(2)}) copy-start(bf16[2560,768]{1,0:T(8,128)(2,1)} %get-tuple-element.1072.g) | copy-start | bytes 11796484 | tf_op jit(solution)/shard_map/while
  838.5 5.7 collective-permute-start.5
  849.9 50.4 %all-to-all-start.3 = ((bf16[2,4,320,768]{3,2,0,1:T(8,128)(2,1)}), bf16[2,4,320,768]{3,2,0,1:T(8,128)(2,1)}, u32[]{:S(2)}, u32[]{:S(2)}) async-start(bf16[2,4,320,768]{3,2,0,1:T(8,128)(2,1)} %copy.73), calls=%async_computation.3 | async-start | bytes 7864320 | tf_op jit(solution)/shard_map/all_to_all | solution.py:341
  (45 other events, 467.8 us)
